TPU v7x, 128 devices: a whole 4x4x4 slice. The times are simulated.
128 devices in a mesh: dp: 16 (over z, y), pp: 8 (over x, core).
Axes of the slice: x: 4, y: 4, z: 4, core: 2. Of those that a mesh axis runs over, the one named last changes fastest.
Arguments:
- tok_ids: int32 [1, 16, 130], P(None, 'dp')
- emb_s: bfloat16 [8, 50304, 1024], P('pp', 'dp')
- w_one: bfloat16 [8, 1, 1024, 4096], P('pp')
- w_two: bfloat16 [8, 1, 4096, 1024], P('pp')
- gain_f: bfloat16 [1024], replicated
- gain_h: bfloat16 [1024], replicated
- gain_e: bfloat16 [1024], replicated
- gain_m: bfloat16 [1024], replicated
- w_proj: bfloat16 [2048, 1024], replicated
- u_one: bfloat16 [1024, 4096], replicated
- u_two: bfloat16 [4096, 1024], replicated
- w_out: bfloat16 [1024, 50304], replicated
Outputs:
- output 1: float32 [], replicated
- output 2: float32 [1, 16, 128], P(None, 'dp')
- output 3: float32 [1, 16, 128], P(None, 'dp')
All inputs are finite; a program needn't handle non-finite values.
Results may differ from a plain program's by a relative error of at most 0.00387627.
Values are sent between devices in bfloat16 or wider.
A program may use at most 1 GiB of HBM per device.

v0:
```python
import jax
import jax.numpy as jnp
from jax import lax
from jax.sharding import PartitionSpec as P

NORM_EPS = 1e-6
MTP_WEIGHT = 0.3
HEAD_ROWS = 128


def norm_plain(x_val):
    x_f = x_val.astype(jnp.float32)
    return (x_f * lax.rsqrt(jnp.mean(x_f * x_f, axis=-1, keepdims=True) + NORM_EPS)).astype(jnp.bfloat16)


def norm_gain(x_val, gain_vec):
    x_f = x_val.astype(jnp.float32)
    scaled = x_f * lax.rsqrt(jnp.mean(x_f * x_f, axis=-1, keepdims=True) + NORM_EPS)
    return (scaled * gain_vec.astype(jnp.float32)).astype(jnp.bfloat16)


def mlp_add(x_val, normed, w_up, w_down):
    hidden = jax.nn.gelu(jnp.dot(normed, w_up, preferred_element_type=jnp.float32)).astype(jnp.bfloat16)
    return (x_val.astype(jnp.float32) + jnp.dot(hidden, w_down, preferred_element_type=jnp.float32)).astype(jnp.bfloat16)


def mtp_depth(h_last, e_rows, gain_h, gain_e, gain_m, w_proj, u_one, u_two):
    row_width = h_last.shape[-1]
    z_sum = jnp.dot(norm_gain(h_last, gain_h), w_proj[:row_width], preferred_element_type=jnp.float32)
    z_sum = z_sum + jnp.dot(norm_gain(e_rows, gain_e), w_proj[row_width:], preferred_element_type=jnp.float32)
    z_val = z_sum.astype(jnp.bfloat16)
    return mlp_add(z_val, norm_gain(z_val, gain_m), u_one, u_two)


def token_nll(normed, targets, w_out):
    n_rows, row_width = normed.shape
    n_blocks = n_rows // HEAD_ROWS

    def one_block(pair):
        block_rows, block_tgt = pair
        logits = jnp.dot(block_rows, w_out, preferred_element_type=jnp.float32)
        picked = jnp.take_along_axis(logits, block_tgt[:, None], axis=1)[:, 0]
        return jax.nn.logsumexp(logits, axis=1) - picked

    per_block = lax.map(one_block, (normed.reshape(n_blocks, HEAD_ROWS, row_width), targets.reshape(n_blocks, HEAD_ROWS)))
    return per_block.reshape(n_rows)


def solution(mesh):
    n_stages = mesh.shape['pp']
    n_data = mesh.shape['dp']
    fwd_perm = [(stage_idx, stage_idx + 1) for stage_idx in range(n_stages - 1)]
    mtp_perm = [(0, n_stages - 1)]

    def body(tok_ids, emb_s, w_one, w_two, gain_f, gain_h, gain_e, gain_m, w_proj, u_one, u_two, w_out):
        stage = lax.axis_index('pp')
        n_micro, batch_dev, seq_plus = tok_ids.shape
        seq_len = seq_plus - 2
        n_layers = w_one.shape[1]
        row_width = w_one.shape[2]
        n_rows = batch_dev * seq_len
        is_first = stage == 0
        is_last = stage == n_stages - 1
        table = lax.all_gather(emb_s[0], 'dp', axis=0, tiled=True)

        def head_losses(h_last, e_rows, ids_out):
            main_nll = token_nll(norm_gain(h_last, gain_f), ids_out[:, 1:seq_len + 1].reshape(n_rows), w_out)
            z_val = mtp_depth(h_last, e_rows, gain_h, gain_e, gain_m, w_proj, u_one, u_two)
            mtp_nll = token_nll(norm_gain(z_val, gain_f), ids_out[:, 2:].reshape(n_rows), w_out)
            return main_nll, mtp_nll

        def no_losses(h_last, e_rows, ids_out):
            zero_rows = jnp.zeros((n_rows,), jnp.float32)
            return zero_rows, zero_rows

        def tick_step(state, t_idx):
            ids_in = lax.dynamic_index_in_dim(tok_ids, jnp.minimum(t_idx, n_micro - 1), axis=0, keepdims=False)
            out_idx = jnp.maximum(t_idx - (n_stages - 1), 0)
            ids_out = lax.dynamic_index_in_dim(tok_ids, out_idx, axis=0, keepdims=False)
            x_val = jnp.where(is_first, table[ids_in[:, :seq_len].reshape(n_rows)], state)
            for layer in range(n_layers):
                x_val = mlp_add(x_val, norm_plain(x_val), w_one[0, layer], w_two[0, layer])
            e_rows = lax.ppermute(table[ids_out[:, 1:seq_len + 1].reshape(n_rows)], 'pp', mtp_perm)
            losses = lax.cond(is_last & (t_idx >= n_stages - 1), head_losses, no_losses, x_val, e_rows, ids_out)
            return lax.ppermute(x_val, 'pp', fwd_perm), losses

        init_state = jnp.zeros((n_rows, row_width), jnp.bfloat16)
        _, (main_all, mtp_all) = lax.scan(tick_step, init_state, jnp.arange(n_micro + n_stages - 1))
        main_nll = lax.psum(main_all[n_stages - 1:], 'pp').reshape(n_micro, batch_dev, seq_len)
        mtp_nll = lax.psum(mtp_all[n_stages - 1:], 'pp').reshape(n_micro, batch_dev, seq_len)
        local_sum = jnp.sum(main_nll) + MTP_WEIGHT * jnp.sum(mtp_nll)
        total_loss = lax.psum(local_sum, 'dp') / (n_micro * batch_dev * n_data * seq_len)
        return total_loss, main_nll, mtp_nll

    replicated = P()
    in_specs = (P(None, 'dp', None), P('pp', 'dp', None), P('pp'), P('pp'), replicated, replicated, replicated, replicated, replicated, replicated, replicated, replicated)
    out_specs = (replicated, P(None, 'dp', None), P(None, 'dp', None))
    return jax.shard_map(body, mesh=mesh, in_specs=in_specs, out_specs=out_specs, check_vma=False)
```

profile of v0, /device:TPU:1, one launch (start us, length us, event | category | flops | bytes accessed | tf_op | source)
XLA Modules:
  0.0 880.7 jit_solution(2787057624696054188)
XLA Ops:
  7.9 0.8 fusion.101
  8.8 555.9 %all-gather.3.cloned.1.call-done = bf16[1,50304,1024]{2,1,0:T(8,128)(2,1)} async-done(((bf16[1,3144,1024]{2,1,0:T(8,128)(2,1)}), bf16[1,50304,1024]{2,1,0:T(8,128)(2,1)}) %all-gather.3.cloned.1.call-update) | async-done | bytes 103022608 | tf_op jit(solution)/shard_map/all_gather | solution.py:64
  564.6 2.2 gather_fusion.3
  567.5 2.2 gather_fusion.2
  569.8 136.7 %while.20 = (s32[]{:T(128)}, bf16[128,1024]{1,0:T(8,128)(2,1)S(1)}, f32[8,128]{1,0:T(8,128)S(1)}, f32[8,128]{1,0:T(8,128)S(1)}, pred[]{:T(512)}, /*index=5*/bf16...) while((s32[]{:T(128)}, bf16[128,1024]{1,0:T(8,128)(2,1)S(1)}, ...), condition=%wide.region_12.14_spmd, body=%wide.region_0.13_spmd.sunk | while | flops 31259734016 | bytes 353714048 | solution.py:88
  570.0 9.3 %fusion.117 = bf16[128,1024]{1,0:T(8,128)(2,1)} fusion(bf16[1,1,4096,1024]{3,2,1,0:T(8,128)(2,1)} %get-tuple-element.670, bf16[1,1,1024,4096]{3,2,1,0:T(8,128)(2,1)} %get-tuple-element.669, f32[128]{0:T(128)S(1)} %add_rsqrt_fusion.6, bf16[128,1024]{1,0:T(8,128)(2,1)S(1)} %get-tuple-element.668, bf16[128,1024]{1,0:T(8,128)(2,1)S(1)} %get-tuple-element.641, ...), kind=kOutput, calls=%fused_computation.102.clone.1 | convolution fusion | flops 2153250816 | bytes 17564160 | tf_op jit(solution)/shard_map/while/body/eval_jaxpr/dot_general | solution.py:24
  579.3 3.9 collective-permute-start
  584.5 2.7 collective-permute-done
  587.4 9.3 %fusion.117 = bf16[128,1024]{1,0:T(8,128)(2,1)} fusion(bf16[1,1,4096,1024]{3,2,1,0:T(8,128)(2,1)} %get-tuple-element.670, bf16[1,1,1024,4096]{3,2,1,0:T(8,128)(2,1)} %get-tuple-element.669, f32[128]{0:T(128)S(1)} %add_rsqrt_fusion.6, bf16[128,1024]{1,0:T(8,128)(2,1)S(1)} %get-tuple-element.668, bf16[128,1024]{1,0:T(8,128)(2,1)S(1)} %get-tuple-element.641, ...), kind=kOutput, calls=%fused_computation.102.clone.1 | convolution fusion | flops 2153250816 | bytes 17564160 | tf_op jit(solution)/shard_map/while/body/eval_jaxpr/dot_general | solution.py:24
  596.7 3.6 collective-permute-start
  601.7 1.9 collective-permute-done
  603.8 9.3 %fusion.117 = bf16[128,1024]{1,0:T(8,128)(2,1)} fusion(bf16[1,1,4096,1024]{3,2,1,0:T(8,128)(2,1)} %get-tuple-element.670, bf16[1,1,1024,4096]{3,2,1,0:T(8,128)(2,1)} %get-tuple-element.669, f32[128]{0:T(128)S(1)} %add_rsqrt_fusion.6, bf16[128,1024]{1,0:T(8,128)(2,1)S(1)} %get-tuple-element.668, bf16[128,1024]{1,0:T(8,128)(2,1)S(1)} %get-tuple-element.641, ...), kind=kOutput, calls=%fused_computation.102.clone.1 | convolution fusion | flops 2153250816 | bytes 17564160 | tf_op jit(solution)/shard_map/while/body/eval_jaxpr/dot_general | solution.py:24
  613.1 4.4 collective-permute-start
  618.8 1.9 collective-permute-done
  620.9 9.3 %fusion.117 = bf16[128,1024]{1,0:T(8,128)(2,1)} fusion(bf16[1,1,4096,1024]{3,2,1,0:T(8,128)(2,1)} %get-tuple-element.670, bf16[1,1,1024,4096]{3,2,1,0:T(8,128)(2,1)} %get-tuple-element.669, f32[128]{0:T(128)S(1)} %add_rsqrt_fusion.6, bf16[128,1024]{1,0:T(8,128)(2,1)S(1)} %get-tuple-element.668, bf16[128,1024]{1,0:T(8,128)(2,1)S(1)} %get-tuple-element.641, ...), kind=kOutput, calls=%fused_computation.102.clone.1 | convolution fusion | flops 2153250816 | bytes 17564160 | tf_op jit(solution)/shard_map/while/body/eval_jaxpr/dot_general | solution.py:24
  630.2 4.4 collective-permute-start
  636.0 1.9 collective-permute-done
  638.1 9.3 %fusion.117 = bf16[128,1024]{1,0:T(8,128)(2,1)} fusion(bf16[1,1,4096,1024]{3,2,1,0:T(8,128)(2,1)} %get-tuple-element.670, bf16[1,1,1024,4096]{3,2,1,0:T(8,128)(2,1)} %get-tuple-element.669, f32[128]{0:T(128)S(1)} %add_rsqrt_fusion.6, bf16[128,1024]{1,0:T(8,128)(2,1)S(1)} %get-tuple-element.668, bf16[128,1024]{1,0:T(8,128)(2,1)S(1)} %get-tuple-element.641, ...), kind=kOutput, calls=%fused_computation.102.clone.1 | convolution fusion | flops 2153250816 | bytes 17564160 | tf_op jit(solution)/shard_map/while/body/eval_jaxpr/dot_general | solution.py:24
  647.4 4.4 collective-permute-start
  653.1 1.9 collective-permute-done
  655.2 9.3 %fusion.117 = bf16[128,1024]{1,0:T(8,128)(2,1)} fusion(bf16[1,1,4096,1024]{3,2,1,0:T(8,128)(2,1)} %get-tuple-element.670, bf16[1,1,1024,4096]{3,2,1,0:T(8,128)(2,1)} %get-tuple-element.669, f32[128]{0:T(128)S(1)} %add_rsqrt_fusion.6, bf16[128,1024]{1,0:T(8,128)(2,1)S(1)} %get-tuple-element.668, bf16[128,1024]{1,0:T(8,128)(2,1)S(1)} %get-tuple-element.641, ...), kind=kOutput, calls=%fused_computation.102.clone.1 | convolution fusion | flops 2153250816 | bytes 17564160 | tf_op jit(solution)/shard_map/while/body/eval_jaxpr/dot_general | solution.py:24
  664.5 4.4 collective-permute-start
  670.3 1.9 collective-permute-done
  672.4 9.3 %fusion.117 = bf16[128,1024]{1,0:T(8,128)(2,1)} fusion(bf16[1,1,4096,1024]{3,2,1,0:T(8,128)(2,1)} %get-tuple-element.670, bf16[1,1,1024,4096]{3,2,1,0:T(8,128)(2,1)} %get-tuple-element.669, f32[128]{0:T(128)S(1)} %add_rsqrt_fusion.6, bf16[128,1024]{1,0:T(8,128)(2,1)S(1)} %get-tuple-element.668, bf16[128,1024]{1,0:T(8,128)(2,1)S(1)} %get-tuple-element.641, ...), kind=kOutput, calls=%fused_computation.102.clone.1 | convolution fusion | flops 2153250816 | bytes 17564160 | tf_op jit(solution)/shard_map/while/body/eval_jaxpr/dot_general | solution.py:24
  681.6 4.4 collective-permute-start
  687.4 1.9 collective-permute-done
  689.5 9.3 %fusion.117 = bf16[128,1024]{1,0:T(8,128)(2,1)} fusion(bf16[1,1,4096,1024]{3,2,1,0:T(8,128)(2,1)} %get-tuple-element.670, bf16[1,1,1024,4096]{3,2,1,0:T(8,128)(2,1)} %get-tuple-element.669, f32[128]{0:T(128)S(1)} %add_rsqrt_fusion.6, bf16[128,1024]{1,0:T(8,128)(2,1)S(1)} %get-tuple-element.668, bf16[128,1024]{1,0:T(8,128)(2,1)S(1)} %get-tuple-element.641, ...), kind=kOutput, calls=%fused_computation.102.clone.1 | convolution fusion | flops 2153250816 | bytes 17564160 | tf_op jit(solution)/shard_map/while/body/eval_jaxpr/dot_general | solution.py:24
  698.8 4.4 collective-permute-start
  704.6 1.9 collective-permute-done
  706.5 131.1 %all-reduce = (f32[1,128]{1,0:T(1,128)S(1)}, f32[1,128]{1,0:T(1,128)S(1)}) all-reduce(f32[1,128]{1,0:T(1,128)S(1)} %slice.30, f32[1,128]{1,0:T(1,128)S(1)} %slice.31), channel_id=1, replica_groups=mesh['dp'=16,'pp'=8] {'pp'}, use_global_device_ids=true, to_apply=%region_13.15 | all-reduce | flops 256 | bytes 2048 | tf_op jit(solution)/shard_map/psum | solution.py:89
  837.6 0.7 reduce_sum.92
  840.2 31.9 %psum.23 = f32[]{:T(128)} all-reduce(f32[]{:T(128)S(6)} %add.154), channel_id=1, replica_groups=mesh['dp'=16,'pp'=8] {'dp'}, use_global_device_ids=true, to_apply=%region_17.19 | all-reduce | flops 1 | bytes 8 | tf_op jit(solution)/shard_map/psum | solution.py:92
  (91 shorter events, 9.1 us)
Async XLA Ops:
  7.2 562.6 %copy-start = (s32[1,1,130]{2,1,0:T(1,128)S(1)}, s32[1,1,130]{2,1,0:T(1,128)}, u32[]{:S(2)}) copy-start(s32[1,1,130]{2,1,0:T(1,128)} %param.18) | copy-start | bytes 1564
  7.2 562.6 %copy-start.1 = (bf16[1024]{0:T(1024)(128)(2,1)S(1)}, bf16[1024]{0:T(1024)(128)(2,1)}, u32[]{:S(2)}) copy-start(bf16[1024]{0:T(1024)(128)(2,1)} %param.22) | copy-start | bytes 6148
  7.2 562.6 %copy-start.2 = (bf16[1024]{0:T(1024)(128)(2,1)S(1)}, bf16[1024]{0:T(1024)(128)(2,1)}, u32[]{:S(2)}) copy-start(bf16[1024]{0:T(1024)(128)(2,1)} %param.23) | copy-start | bytes 6148
  7.2 562.6 %copy-start.3 = (bf16[1024]{0:T(1024)(128)(2,1)S(1)}, bf16[1024]{0:T(1024)(128)(2,1)}, u32[]{:S(2)}) copy-start(bf16[1024]{0:T(1024)(128)(2,1)} %param.24) | copy-start | bytes 6148
  7.2 562.6 %copy-start.4 = (bf16[1024]{0:T(1024)(128)(2,1)S(1)}, bf16[1024]{0:T(1024)(128)(2,1)}, u32[]{:S(2)}) copy-start(bf16[1024]{0:T(1024)(128)(2,1)} %param.25) | copy-start | bytes 6148
  7.2 557.4 %all-gather.3.cloned.1.call-start = ((), (), s32[]{:S(2)}) async-start(), calls=%async_computation | async-start | bytes 109461504 | tf_op jit(solution)/shard_map/all_gather | solution.py:64
  566.8 2.9 collective-permute-start.1
  579.3 7.9 collective-permute-start
  596.7 6.9 collective-permute-start
  613.1 7.7 collective-permute-start
  630.2 7.7 collective-permute-start
  647.4 7.7 collective-permute-start
  664.5 7.7 collective-permute-start
  681.6 7.7 collective-permute-start
  698.8 7.7 collective-permute-start
  837.6 35.2 %copy-start.5 = (f32[1,128]{1,0:T(1,128)}, f32[1,128]{1,0:T(1,128)S(1)}, u32[]{:S(2)}) copy-start(f32[1,128]{1,0:T(1,128)S(1)} %get-tuple-element.466) | copy-start | bytes 1540
  837.6 35.2 %copy-start.6 = (f32[1,128]{1,0:T(1,128)}, f32[1,128]{1,0:T(1,128)S(1)}, u32[]{:S(2)}) copy-start(f32[1,128]{1,0:T(1,128)S(1)} %get-tuple-element.467) | copy-start | bytes 1540
Sparse Core Ops, SparseCore 0:
  10.2 554.4 all-gather.2
where the time goes:
time: 891 us; the launch traced here: 881 us
  waiting for transfers between devices  573 us (64%)
  blocking collectives  163 us (18%)
  matrix products  74.3 us (8%)
  starting transfers between devices  34.7 us (4%)
  between operations  17.3 us (2%)
  local copies, waits for them, and re-layouts  9.71 us (1%)
    all_gather x1, waiting for transfers between devices, body(): table = lax.all_gather(emb_s[0], 'dp', axis=0, tiled=True)  556 us
    psum x1, blocking collectives, body(): lax.psum(main_all[n_stages - 1:], 'pp').reshape(n_micro, batch_dev, seq_len)  131 us
    dot_general x8, matrix products, mlp_add(): jnp.dot(hidden, w_down, preferred_element_type=jnp.float32)  74.3 us
    ppermute x8, starting transfers between devices, tick_step(): return (lax.ppermute(x_val, 'pp', fwd_perm), losses)  33.9 us
    psum x1, blocking collectives, body(): lax.psum(local_sum, 'dp') / (n_micro * batch_dev * n_data * seq_len)  31.9 us
  transfers between devices with their start and end apart: 10, of which 9 were waited for; matrix products, arithmetic and copies ran while one was open for 1% of the time, Pallas kernels for 0%

commit v1 on v0

v1 whole, which is shorter than its diff:
```python
import functools

import jax
import jax.numpy as jnp
from jax import lax
from jax.experimental import pallas as pl
from jax.experimental.pallas import tpu as pltpu
from jax.sharding import PartitionSpec as P

NORM_EPS = 1e-6
MTP_WEIGHT = 0.3
HEAD_ROWS = 128
LANES = 128
SUB = 8
ID_PAD = 256
CAP = 24
PIECE = 256
MLP_BLOCK = 1024
VMEM_LIMIT = 66_900_000
F32 = jnp.float32
BF16 = jnp.bfloat16
MESH = pl.DeviceIdType.MESH


def norm_f32(x_f):
    return x_f * lax.rsqrt(jnp.mean(x_f * x_f, axis=-1, keepdims=True) + NORM_EPS)


def iota(shape, dim):
    return lax.broadcasted_iota(jnp.int32, shape, dim)


def dot32(a, b):
    return jnp.dot(a, b, preferred_element_type=F32)


def mega_kernel(
    n_dp, n_pp, seq, cap,
    ids_ref, gains_ref, emb, w1h, w2h, wph, u1h, u2h, woh,
    main_out, mtp_out, loss_out, flag_out,
    w1, w2, u1, u2, wp, wo,
    ids_all, send_rows, recv_rows, xbuf, ybuf, xnb, hid, ebuf, hbuf, eall, zbuf, epart, xh, lg, mx, sm, pk,
    part_send, part_recv, ls_send, ls_recv,
    wsem, ids_ss, ids_rs, row_ss, row_rs, x_ss, x_rs, e_ss, e_rs, h_ss, h_rs, f_ss, part_ss, part_rs, ls_ss, ls_rs,
):
    d = lax.axis_index("dp")
    p = lax.axis_index("pp")
    width = xbuf.shape[1]
    ffn = w1.shape[1]
    n_rows = emb.shape[1]
    half = seq // 2
    n_shard = n_pp // 2
    shard = lax.rem(p, n_shard)
    group = p // n_shard
    n_tiles = woh.shape[1] // LANES
    base_tiles = n_tiles // n_shard
    cols = w1.shape[1] + wo.shape[1]
    own_cols = wo.shape[1]
    n_piece = width // PIECE
    is_first = p == 0
    is_last = p == n_pp - 1
    k_main = n_rows // ID_PAD * ID_PAD
    k_pad = k_main + ID_PAD

    col0 = pl.multiple_of(shard * (base_tiles * LANES), LANES)
    tab_cp = pltpu.make_async_copy(emb.at[0], u2.at[pl.ds(0, n_rows), :], wsem.at[0])
    w1_cp = pltpu.make_async_copy(w1h.at[0, 0], w1, wsem.at[1])
    w2_cp = pltpu.make_async_copy(w2h.at[0, 0], w2, wsem.at[2])
    u1_cp = pltpu.make_async_copy(u1h, u1, wsem.at[3])
    u2_cp = pltpu.make_async_copy(u2h, u2, wsem.at[4])
    wp_cp = pltpu.make_async_copy(wph, wp, wsem.at[5])
    wo_cp = pltpu.make_async_copy(woh.at[:, pl.ds(col0 + ffn, own_cols)], wo, wsem.at[6])
    late_cp = pltpu.make_async_copy(woh.at[:, pl.ds(col0, ffn)], w1, wsem.at[7])

    @pl.when(is_first)
    def _():
        tab_cp.start()

    @pl.when(jnp.logical_not(is_first))
    def _():
        w1_cp.start()
        w2_cp.start()

    barrier = pltpu.get_barrier_semaphore()
    for k in range(1, n_dp):
        pl.semaphore_signal(barrier, inc=1, device_id={"dp": lax.rem(d + k, n_dp)}, device_id_type=MESH)
    for k in range(1, n_pp):
        pl.semaphore_signal(barrier, inc=1, device_id={"pp": lax.rem(p + k, n_pp)}, device_id_type=MESH)
    pl.semaphore_wait(barrier, n_dp - 1 + n_pp - 1)

    def ids_copy(owner, peer):
        return pltpu.make_async_remote_copy(
            src_ref=ids_ref, dst_ref=ids_all.at[owner], send_sem=ids_ss.at[peer], recv_sem=ids_rs.at[owner],
            device_id={"dp": peer}, device_id_type=MESH)

    for k in range(1, n_dp):
        ids_copy(d, lax.rem(d + k, n_dp)).start()
    ids_all[d] = ids_ref[...]

    @pl.when(jnp.logical_not(is_first))
    def _():
        u1_cp.start()
        u2_cp.start()
        wp_cp.start()
        wo_cp.start()

    for k in range(1, n_dp):
        peer = lax.rem(d + k, n_dp)
        ids_copy(peer, peer).wait_recv()

    def set_flag():
        ids2 = ids_all[...].reshape(n_dp * SUB, ID_PAD)
        used = iota((n_dp * SUB, ID_PAD), 1) < seq + 1
        most = jnp.zeros((n_dp * SUB, 1), F32)
        for k in range(n_dp):
            hit = (ids2 >= k * n_rows) & (ids2 < (k + 1) * n_rows) & used
            most = jnp.maximum(most, jnp.sum(jnp.where(hit, 1.0, 0.0), axis=1, keepdims=True))
        over = jnp.max(most, axis=0, keepdims=True)
        flag_out[...] = jnp.broadcast_to(jnp.where(over > cap, 1.0, 0.0), (SUB, LANES))

    def row_copy(owner, peer):
        return pltpu.make_async_remote_copy(
            src_ref=send_rows.at[peer], dst_ref=recv_rows.at[owner], send_sem=row_ss.at[peer], recv_sem=row_rs.at[owner],
            device_id={"dp": peer}, device_id_type=MESH)

    @pl.when(is_first)
    def _():
        w1_cp.start()
        w2_cp.start()
        low = d * n_rows
        ids2 = ids_all[...].reshape(n_dp * SUB, ID_PAD)
        lane2 = iota((n_dp * SUB, ID_PAD), 1)
        valid = (ids2 >= low) & (ids2 < low + n_rows) & (lane2 < seq + 1)
        before = jnp.where(iota((ID_PAD, ID_PAD), 0) < iota((ID_PAD, ID_PAD), 1), 1.0, 0.0).astype(BF16)
        rank = dot32(jnp.where(valid, 1.0, 0.0).astype(BF16), before)
        key = jnp.where(valid, rank, -1.0)
        loc = jnp.where(valid, ids2 - low, 0).astype(F32)
        slot = iota((cap, ID_PAD), 0).astype(F32)
        for b in range(0, n_dp, 2):
            picks = []
            for s in (b, b + 1):
                sel = key[s * SUB:s * SUB + 1, :] == slot
                idx = jnp.sum(jnp.where(sel, loc[s * SUB:s * SUB + 1, :] + 1.0, 0.0), axis=1, keepdims=True) - 1.0
                picks.append(idx)
            idx2 = jnp.concatenate(picks, axis=0).astype(jnp.int32)
            hot = jnp.where(iota((2 * cap, k_pad), 1) == idx2, 1.0, 0.0).astype(BF16)
            u1[b * cap:(b + 2) * cap, 0:k_pad] = hot
        tab_cp.wait()
        n_slots = n_dp * cap
        blk = min(512, width)
        for c in range(0, width, blk):
            tail = u2[k_main:k_pad, c:c + blk]
            tail = jnp.where(iota((ID_PAD, blk), 0) < n_rows - k_main, tail.astype(F32), 0.0).astype(BF16)
            got = dot32(u1[0:n_slots, 0:k_main], u2[0:k_main, c:c + blk]) + dot32(u1[0:n_slots, k_main:k_pad], tail)
            for s in range(n_dp):
                send_rows[s, :, c:c + blk] = got[s * cap:(s + 1) * cap, :].astype(BF16)
        for k in range(1, n_dp):
            row_copy(d, lax.rem(d + k, n_dp)).start()
        recv_rows[d] = send_rows[d]
        u1_cp.start()
        u2_cp.start()
        wp_cp.start()
        wo_cp.start()
        row = ids_ref[0:1, :]
        rr = iota((2 * seq, ID_PAD), 0)
        ll = iota((2 * seq, ID_PAD), 1)
        pos = jnp.where(rr < seq, rr, rr - seq + 1)
        id_col = jnp.sum(jnp.where(ll == pos, jnp.broadcast_to(row, (2 * seq, ID_PAD)), 0).astype(F32), axis=1, keepdims=True)
        src_col = jnp.zeros((2 * seq, 1), F32)
        src_row = jnp.zeros((1, ID_PAD), F32)
        for k in range(1, n_dp):
            src_col = src_col + jnp.where(id_col >= float(k * n_rows), 1.0, 0.0)
            src_row = src_row + jnp.where(row >= k * n_rows, 1.0, 0.0)
        earlier = (jnp.broadcast_to(src_row, (2 * seq, ID_PAD)) == src_col) & (ll < pos)
        rank_col = jnp.sum(jnp.where(earlier, 1.0, 0.0), axis=1, keepdims=True)
        where_col = jnp.where(rank_col < float(cap), src_col * float(cap) + rank_col, -1.0).astype(jnp.int32)
        place = jnp.where(iota((2 * seq, n_slots), 1) == where_col, 1.0, 0.0).astype(BF16)
        for k in range(1, n_dp):
            peer = lax.rem(d + k, n_dp)
            row_copy(peer, peer).wait_recv()
        rows = dot32(place, recv_rows[...].reshape(n_slots, width)).astype(BF16)
        xbuf[...] = rows[0:seq, :]
        eall[...] = rows[seq:2 * seq, :]

    @pl.when(jnp.logical_not(is_first))
    def _():
        set_flag()

    def x_copy(i):
        part = pl.ds(i * PIECE, PIECE)
        return pltpu.make_async_remote_copy(
            src_ref=ybuf.at[:, part], dst_ref=xbuf.at[:, part], send_sem=x_ss.at[i], recv_sem=x_rs.at[i],
            device_id={"pp": lax.rem(p + 1, n_pp)}, device_id_type=MESH)

    h_peers = ((1, 0), (3, 0), (5, half), (6, half))

    def h_copy(j, i):
        to, row0 = h_peers[j]
        part = pl.ds(i * PIECE, PIECE)
        return pltpu.make_async_remote_copy(
            src_ref=ybuf.at[pl.ds(row0, half), part], dst_ref=hbuf.at[:, part], send_sem=h_ss.at[j, i], recv_sem=h_rs.at[i],
            device_id={"pp": to}, device_id_type=MESH)

    def f_copy(i):
        part = pl.ds(i * PIECE, PIECE)
        return pltpu.make_async_remote_copy(
            src_ref=hbuf.at[:, part], dst_ref=hbuf.at[:, part], send_sem=f_ss.at[i], recv_sem=h_rs.at[i],
            device_id={"pp": lax.rem(p + n_pp - 1, n_pp)}, device_id_type=MESH)

    def gelu_up(m, xn, w_up):
        for c in range(0, ffn, MLP_BLOCK):
            hid[0:m, c:c + MLP_BLOCK] = jax.nn.gelu(dot32(xn, w_up[:, c:c + MLP_BLOCK])).astype(BF16)

    w1_cp.wait()

    @pl.when(jnp.logical_not(is_first))
    def _():
        for i in range(n_piece):
            x_copy(i).wait_recv()

    xnb[...] = norm_f32(xbuf[...].astype(F32)).astype(BF16)
    gelu_up(seq, xnb[...], w1)
    w2_cp.wait()
    for i in range(n_piece):
        c = i * PIECE
        out = xbuf[:, c:c + PIECE].astype(F32) + dot32(hid[...], w2[:, c:c + PIECE])
        ybuf[:, c:c + PIECE] = out.astype(BF16)

        @pl.when(jnp.logical_not(is_last))
        def _():
            x_copy(i).start()

        @pl.when(is_last)
        def _():
            for j in range(len(h_peers)):
                h_copy(j, i).start()

    late_cp.start()

    def e_copy(to):
        row0 = half * (to // n_shard)
        return pltpu.make_async_remote_copy(
            src_ref=eall.at[pl.ds(row0, half), :], dst_ref=ebuf, send_sem=e_ss.at[to], recv_sem=e_rs,
            device_id={"pp": to}, device_id_type=MESH)

    @pl.when(is_first)
    def _():
        for to in range(1, n_pp):
            e_copy(to).start()
        ebuf[...] = eall[0:half, :]
        set_flag()

    @pl.when(jnp.logical_not(is_first))
    def _():
        e_copy(1).wait_recv()

    g_f = gains_ref[0:1, :]
    g_h = gains_ref[1:2, :]
    g_e = gains_ref[2:3, :]
    g_m = gains_ref[3:4, :]

    wp_cp.wait()
    e_n = (norm_f32(ebuf[...].astype(F32)) * g_e).astype(BF16)
    epart[...] = dot32(e_n, wp[width:2 * width, :])
    u1_cp.wait()
    u2_cp.wait()
    wo_cp.wait()

    row_f = jnp.broadcast_to(ids_ref[0:1, :], (2 * half, ID_PAD))
    rr = iota((2 * half, ID_PAD), 0)
    at = jnp.where(rr < half, rr + 1, rr - half + 2) + group * half
    tgt = jnp.sum(jnp.where(iota((2 * half, ID_PAD), 1) == at, row_f, 0).astype(F32), axis=1, keepdims=True)
    tgt = tgt.astype(jnp.int32) - shard * (base_tiles * LANES)
    tgt = jnp.broadcast_to(tgt, (2 * half, LANES))

    @pl.when(is_last)
    def _():
        hbuf[...] = ybuf[half:seq, :]

    @pl.when(jnp.logical_not(is_last))
    def _():
        for i in range(n_piece):
            h_copy(0, i).wait_recv()

            @pl.when((p == 1) | (p == 3) | (p == 5))
            def _():
                f_copy(i).start()

    h_f = norm_f32(hbuf[...].astype(F32))
    z_val = (dot32((h_f * g_h).astype(BF16), wp[0:width, :]) + epart[...]).astype(BF16)
    zbuf[...] = z_val
    xh[0:half, :] = (h_f * g_f).astype(BF16)
    xnb[0:half, :] = (norm_f32(z_val.astype(F32)) * g_m).astype(BF16)
    gelu_up(half, xnb[0:half, :], u1)
    z_out = (zbuf[...].astype(F32) + dot32(hid[0:half, :], u2[...])).astype(BF16)
    xh[half:2 * half, :] = (norm_f32(z_out.astype(F32)) * g_f).astype(BF16)

    lane = iota((2 * half, LANES), 1)
    tail_ok = jnp.broadcast_to(shard == n_shard - 1, (2 * half, LANES))
    blocks = [(wo, c, ffn + c, min(MLP_BLOCK, own_cols - c)) for c in range(0, own_cols, MLP_BLOCK)]
    blocks += [(w1, c, c, MLP_BLOCK) for c in range(0, ffn, MLP_BLOCK)]

    def logits_of(i):
        ref, c, _, n = blocks[i]
        lg[i % 2, :, 0:n] = dot32(xh[...], ref[:, c:c + n])

    def fold(i):
        _, _, start, n = blocks[i]
        tiles = []
        for t in range(0, n, LANES):
            val = lg[i % 2, :, t:t + LANES]
            tiles.append((start + t, val, start + t == cols - LANES))
        top = None if i == 0 else mx[...]
        for _, val, last in tiles:
            val = jnp.where(tail_ok, val, -jnp.inf) if last else val
            top = val if top is None else jnp.maximum(top, val)
        total = jnp.zeros_like(top) if i == 0 else sm[...] * jnp.exp(mx[...] - top)
        hit = jnp.zeros_like(top) if i == 0 else pk[...]
        for at_col, val, last in tiles:
            e_val = jnp.exp(val - top)
            match = lane == tgt - at_col
            if last:
                e_val = jnp.where(tail_ok, e_val, 0.0)
                match = match & tail_ok
            total = total + e_val
            hit = hit + jnp.where(match, val, 0.0)
        mx[...] = top
        sm[...] = total
        pk[...] = hit

    for i in range(len(blocks)):
        if i == len(blocks) - ffn // MLP_BLOCK:
            late_cp.wait()
        logits_of(i)
        if i:
            fold(i - 1)
    fold(len(blocks) - 1)

    eye = iota((2 * half, LANES), 0) == iota((2 * half, LANES), 1)

    def as_row(col):
        return jnp.sum(jnp.where(eye, jnp.broadcast_to(col, (2 * half, LANES)), 0.0), axis=0, keepdims=True)

    top = mx[...]
    m_col = jnp.max(top, axis=1, keepdims=True)
    s_col = jnp.sum(sm[...] * jnp.exp(top - m_col), axis=1, keepdims=True)
    p_col = jnp.sum(pk[...], axis=1, keepdims=True)
    sub = iota((SUB, LANES), 0)
    tile = jnp.where(sub == 0, as_row(m_col), jnp.where(sub == 1, as_row(s_col), as_row(p_col)))
    part_send[...] = tile
    part_recv[p] = tile

    def part_copy(owner, peer):
        return pltpu.make_async_remote_copy(
            src_ref=part_send, dst_ref=part_recv.at[owner], send_sem=part_ss.at[peer], recv_sem=part_rs.at[owner],
            device_id={"pp": peer}, device_id_type=MESH)

    for k in range(1, n_pp):
        part_copy(p, lax.rem(p + k, n_pp)).start()
    for k in range(1, n_pp):
        peer = lax.rem(p + k, n_pp)
        part_copy(peer, peer).wait_recv()

    def group_nll(g):
        got = [part_recv[g * n_shard + i] for i in range(n_shard)]
        best = functools.reduce(jnp.maximum, [t[0:1, :] for t in got])
        total = sum(t[1:2, :] * jnp.exp(t[0:1, :] - best) for t in got)
        return best + jnp.log(total) - sum(t[2:3, :] for t in got)

    nll_a = jnp.broadcast_to(group_nll(0), (SUB, LANES))
    nll_b = jnp.broadcast_to(group_nll(1), (SUB, LANES))
    low_lane = iota((SUB, LANES), 1) < half
    main = jnp.where(low_lane, nll_a, pltpu.roll(nll_b, half, 1))
    mtp = jnp.where(low_lane, pltpu.roll(nll_a, half, 1), nll_b)
    main_out[...] = main[0:1, :]
    mtp_out[...] = mtp[0:1, :]
    both = main + MTP_WEIGHT * mtp
    ls_send[...] = both
    ls_recv[d] = both

    def ls_copy(owner, peer):
        return pltpu.make_async_remote_copy(
            src_ref=ls_send, dst_ref=ls_recv.at[owner], send_sem=ls_ss.at[peer], recv_sem=ls_rs.at[owner],
            device_id={"dp": peer}, device_id_type=MESH)

    for k in range(1, n_dp):
        ls_copy(d, lax.rem(d + k, n_dp)).start()
    for k in range(1, n_dp):
        peer = lax.rem(d + k, n_dp)
        ls_copy(peer, peer).wait_recv()
    acc = ls_recv[0]
    for k in range(1, n_dp):
        acc = acc + ls_recv[k]
    loss_out[...] = jnp.broadcast_to(jnp.sum(acc, axis=1, keepdims=True) * (1.0 / (n_dp * seq)), (SUB, LANES))

    for k in range(1, n_dp):
        peer = lax.rem(d + k, n_dp)
        ids_copy(d, peer).wait_send()
        ls_copy(d, peer).wait_send()
    for k in range(1, n_pp):
        part_copy(p, lax.rem(p + k, n_pp)).wait_send()

    @pl.when(is_first)
    def _():
        for k in range(1, n_dp):
            row_copy(d, lax.rem(d + k, n_dp)).wait_send()
        for to in range(1, n_pp):
            e_copy(to).wait_send()

    @pl.when(jnp.logical_not(is_last))
    def _():
        for i in range(n_piece):
            x_copy(i).wait_send()

    @pl.when((p == 1) | (p == 3) | (p == 5))
    def _():
        for i in range(n_piece):
            f_copy(i).wait_send()

    @pl.when(is_last)
    def _():
        for j in range(len(h_peers)):
            for i in range(n_piece):
                h_copy(j, i).wait_send()


def mega(n_dp, n_pp, seq, ids, gains, emb, w1, w2, wp, u1, u2, wo):
    width, ffn = w1.shape[2], w1.shape[3]
    n_tiles = wo.shape[1] // LANES
    n_shard = n_pp // 2
    cols = (n_tiles - (n_shard - 1) * (n_tiles // n_shard)) * LANES
    half = seq // 2
    n_piece = width // PIECE
    dma = pltpu.SemaphoreType.DMA
    tile = pltpu.VMEM((SUB, LANES), F32)
    vmem = pl.BlockSpec(memory_space=pltpu.VMEM)
    anys = pl.BlockSpec(memory_space=pl.ANY)
    act = pltpu.VMEM((seq, width), BF16)
    act_half = pltpu.VMEM((half, width), BF16)
    return pl.pallas_call(
        functools.partial(mega_kernel, n_dp, n_pp, seq, CAP),
        out_shape=(
            jax.ShapeDtypeStruct((1, seq), F32),
            jax.ShapeDtypeStruct((1, seq), F32),
            jax.ShapeDtypeStruct((SUB, LANES), F32),
            jax.ShapeDtypeStruct((SUB, LANES), F32),
        ),
        in_specs=[vmem] * 2 + [anys] * 7,
        out_specs=(vmem,) * 4,
        scratch_shapes=[
            pltpu.VMEM((width, ffn), BF16),
            pltpu.VMEM((ffn, width), BF16),
            pltpu.VMEM((width, ffn), BF16),
            pltpu.VMEM((ffn, width), BF16),
            pltpu.VMEM((2 * width, width), BF16),
            pltpu.VMEM((width, cols - ffn), BF16),
            pltpu.VMEM((n_dp, SUB, ID_PAD), jnp.int32),
            pltpu.VMEM((n_dp, CAP, width), BF16),
            pltpu.VMEM((n_dp, CAP, width), BF16),
            act, act, act,
            pltpu.VMEM((seq, ffn), BF16),
            act_half, act_half,
            act,
            act_half,
            pltpu.VMEM((half, width), F32),
            act,
            pltpu.VMEM((2, 2 * half, MLP_BLOCK), F32),
            pltpu.VMEM((2 * half, LANES), F32), pltpu.VMEM((2 * half, LANES), F32), pltpu.VMEM((2 * half, LANES), F32),
            tile, pltpu.VMEM((n_pp, SUB, LANES), F32),
            tile, pltpu.VMEM((n_dp, SUB, LANES), F32),
            dma((8,)), dma((n_dp,)), dma((n_dp,)), dma((n_dp,)), dma((n_dp,)),
            dma((n_piece,)), dma((n_piece,)), dma((n_pp,)), dma(()), dma((4, n_piece)), dma((n_piece,)), dma((n_piece,)),
            dma((n_pp,)), dma((n_pp,)), dma((n_dp,)), dma((n_dp,)),
        ],
        compiler_params=pltpu.CompilerParams(collective_id=0, has_side_effects=True, vmem_limit_bytes=VMEM_LIMIT),
        name="mtp_eval",
    )(ids, gains, emb, w1, w2, wp, u1, u2, wo)


def norm_plain(x_val):
    return norm_f32(x_val.astype(F32)).astype(BF16)


def norm_gain(x_val, gain_vec):
    return (norm_f32(x_val.astype(F32)) * gain_vec.astype(F32)).astype(BF16)


def mlp_add(x_val, normed, w_up, w_down):
    hidden = jax.nn.gelu(dot32(normed, w_up)).astype(BF16)
    return (x_val.astype(F32) + dot32(hidden, w_down)).astype(BF16)


def token_nll(normed, targets, w_out):
    n_rows, row_width = normed.shape
    n_blocks = n_rows // HEAD_ROWS

    def one_block(pair):
        block_rows, block_tgt = pair
        logits = dot32(block_rows, w_out)
        picked = jnp.take_along_axis(logits, block_tgt[:, None], axis=1)[:, 0]
        return jax.nn.logsumexp(logits, axis=1) - picked

    per_block = lax.map(one_block, (normed.reshape(n_blocks, HEAD_ROWS, row_width), targets.reshape(n_blocks, HEAD_ROWS)))
    return per_block.reshape(n_rows)


def any_ids(n_dp, n_pp, seq, ids, emb, w_one, w_two, gain_f, gain_h, gain_e, gain_m, w_proj, u_one, u_two, w_out):
    stage = lax.axis_index("pp")
    me = lax.axis_index("dp")
    n_rows, width = emb.shape
    ring = [(i, (i + 1) % n_dp) for i in range(n_dp)]
    want = ids[:seq + 1]

    def take(k, held, rows):
        local = want - lax.rem(me - k + n_dp, n_dp) * n_rows
        here = (local >= 0) & (local < n_rows)
        return jnp.where(here[:, None], held[jnp.clip(local, 0, n_rows - 1)], rows)

    def gather_step(k, carry):
        held, rows = carry
        rows = take(k, held, rows)
        return lax.ppermute(held, "dp", ring), rows

    rows = take(0, emb, jnp.zeros((seq + 1, width), BF16))
    _, rows = lax.fori_loop(1, n_dp, gather_step, (lax.ppermute(emb, "dp", ring), rows))
    to_next = [(i, i + 1) for i in range(n_pp - 1)]

    def tick(k, carry):
        x_val, _ = carry
        x_val = jnp.where((stage == 0) & (k == 0), rows[:seq], x_val)
        y_val = mlp_add(x_val, norm_plain(x_val), w_one, w_two)
        return lax.ppermute(y_val, "pp", to_next), y_val

    zero = jnp.zeros((seq, width), BF16)
    _, h_last = lax.fori_loop(0, n_pp, tick, (zero, zero))
    e_rows = lax.ppermute(rows[1:seq + 1], "pp", [(0, n_pp - 1)])
    main_nll = token_nll(norm_gain(h_last, gain_f), ids[1:seq + 1], w_out)
    z_sum = dot32(norm_gain(h_last, gain_h), w_proj[:width]) + dot32(norm_gain(e_rows, gain_e), w_proj[width:])
    z_val = z_sum.astype(BF16)
    z_val = mlp_add(z_val, norm_gain(z_val, gain_m), u_one, u_two)
    mtp_nll = token_nll(norm_gain(z_val, gain_f), ids[2:], w_out)
    is_last = stage == n_pp - 1
    main_nll = lax.psum(jnp.where(is_last, main_nll, 0.0), "pp")
    mtp_nll = lax.psum(jnp.where(is_last, mtp_nll, 0.0), "pp")
    total = lax.psum(jnp.sum(main_nll) + MTP_WEIGHT * jnp.sum(mtp_nll), "dp") / (n_dp * seq)
    return total, main_nll.reshape(1, seq), mtp_nll.reshape(1, seq)


def solution(mesh):
    n_pp = mesh.shape["pp"]
    n_dp = mesh.shape["dp"]

    def body(tok_ids, emb_s, w_one, w_two, gain_f, gain_h, gain_e, gain_m, w_proj, u_one, u_two, w_out):
        seq = tok_ids.shape[2] - 2
        ids = tok_ids.reshape(1, seq + 2)
        ids_pad = jnp.pad(jnp.broadcast_to(ids, (SUB, seq + 2)), ((0, 0), (0, ID_PAD - seq - 2)), constant_values=-1)
        gains = jnp.stack([gain_f, gain_h, gain_e, gain_m] * 2).astype(F32)
        main_nll, mtp_nll, total, over = mega(n_dp, n_pp, seq, ids_pad, gains, emb_s, w_one, w_two, w_proj, u_one, u_two, w_out)

        def slow():
            return any_ids(n_dp, n_pp, seq, ids[0], emb_s[0], w_one[0, 0], w_two[0, 0], gain_f, gain_h, gain_e, gain_m,
                           w_proj, u_one, u_two, w_out)

        def fast():
            return total[0, 0], main_nll, mtp_nll

        loss, main_nll, mtp_nll = lax.cond(over[0, 0] > 0.0, slow, fast)
        return loss, main_nll.reshape(1, 1, seq), mtp_nll.reshape(1, 1, seq)

    rep = P()
    in_specs = (P(None, "dp", None), P("pp", "dp", None), P("pp"), P("pp"), rep, rep, rep, rep, rep, rep, rep, rep)
    out_specs = (rep, P(None, "dp", None), P(None, "dp", None))
    return jax.shard_map(body, mesh=mesh, in_specs=in_specs, out_specs=out_specs, check_vma=False)
```

time: 891 us -> 111 us (0.12); the launches traced: 881 us -> 110 us
  waiting for transfers between devices: 573 us -> 0 us
  blocking collectives: 163 us -> 0 us
  Pallas kernels: 0 us -> 100 us
  matrix products: 74.3 us -> 0 us
  starting transfers between devices: 34.7 us -> 0 us
  between operations: 17.3 us -> 1.35 us
    all_gather x1 -> x0, waiting for transfers between devices: 556 us -> none  [body(): table = lax.all_gather(emb_s[0], 'dp', axis=0, tiled=True)]
    psum x2 -> x0, blocking collectives: 163 us -> none  [the longest x1 131 us: body(): lax.psum(main_all[n_stages - 1:], 'pp').reshape(n_micro, batch_dev, seq_len)]
    pallas_call x0 -> x1, Pallas kernels: none -> 100 us  [mega(): pl.pallas_call(functools.partial(mega_kernel, n_dp, n_pp, seq, CAP), out_...]
    dot_general x8 -> x0, matrix products: 74.3 us -> none  [mlp_add(): jnp.dot(hidden, w_down, preferred_element_type=jnp.float32)]
    ppermute x9 -> x0, starting transfers between devices: 34.6 us -> none  [the longest x8 33.9 us: tick_step(): return (lax.ppermute(x_val, 'pp', fwd_perm), losses)]
    ppermute x9 -> x0, waiting for transfers between devices: 16.1 us -> none  [the longest x8 16.1 us: tick_step(): return (lax.ppermute(x_val, 'pp', fwd_perm), losses)]
  transfers between devices with their start and end apart: 10 -> 0, of which waited for: 9 -> 0; matrix products, arithmetic and copies ran while one was open for 1% -> 0% of each run, Pallas kernels for 0% -> 0%
where the time goes in v1:
time: 111 us; the launch traced here: 110 us
  Pallas kernels  100 us (90%)
  local copies, waits for them, and re-layouts  8.05 us (7%)
  between operations  1.35 us (1%)
    pallas_call x1, Pallas kernels, mega(): pl.pallas_call(functools.partial(mega_kernel, n_dp, n_pp, seq, CAP), out_...  100 us
    another operation x5, local copies, waits for them, and re-layouts, body(): gains = jnp.stack([gain_f, gain_h, gain_e, gain_m] * 2).astype(F32)  2.8 us
    unnamed x12, local copies, waits for them, and re-layouts  2.27 us

profile of v1, /device:TPU:1, one launch (start us, length us, event | category | flops | bytes accessed | tf_op | source)
XLA Modules:
  0.0 110.4 jit_solution(8829835372123835125)
XLA Ops:
  0.6 0.7 pad.6
  1.3 0.7 stack.19
  2.0 0.7 stack.20
  2.7 0.7 stack.21
  3.4 0.7 stack.22
  4.1 0.1 stack.23
  4.1 0.6 pad.7.ids_ref
  4.7 0.6 convert_element_type.97.gains_ref
  5.3 0.0 copy-start.2
  5.3 0.0 copy-start.3
  5.3 0.0 copy-start.4
  5.3 0.0 copy-start.5
  5.3 0.0 copy-start.6
  5.3 100.3 %mtp_eval.1 = (f32[1,128]{1,0:T(1,128)}, f32[1,128]{1,0:T(1,128)}, f32[8,128]{1,0:T(8,128)S(1)}, f32[8,128]{1,0:T(8,128)}) custom-call(s32[8,256]{1,0:T(8,128)} %pad.7.ids_ref, f32[8,1024]{1,0:T(8,128)} %convert_element_type.97.gains_ref, bf16[1,3144,1024]{2,1,0:T(8,128)(2,1)} %emb.1, bf16[1,1,1024,4096]{3,2,1,0:T(8,128)(2,1)} %w1h.1, ...), custom_call_target="tpu_custom_call" | custom-call | tf_op jit(solution)/shard_map/mtp_eval/pallas_call | solution.py:440
  105.7 1.2 %slice.38 = f32[1,1]{1,0:T(1,128)} slice(f32[8,128]{1,0:T(8,128)} %get-tuple-element.343), slice={[0:1], [0:1]} | slice | bytes 8 | tf_op jit(solution)/shard_map/slice | solution.py:567
  107.5 0.0 copy-done.2
  107.5 0.0 copy-done.3
  107.6 0.0 copy-done.4
  107.6 0.0 copy-done.5
  107.6 0.0 copy-done.6
  107.6 0.5 conditional.1
  107.6 0.5 slice.28
  108.1 1.1 %copy.41 = f32[1,1,128]{2,1,0:T(1,128)} copy(f32[1,1,128]{2,1,0:T(1,128)} %bitcast.83) | data formatting | bytes 1024
  109.2 1.1 %copy.42 = f32[1,1,128]{2,1,0:T(1,128)} copy(f32[1,1,128]{2,1,0:T(1,128)} %bitcast.85) | data formatting | bytes 1024
Async XLA Ops:
  5.3 102.2 %copy-start.2 = (s32[1,1,130]{2,1,0:T(1,128)S(1)}, s32[1,1,130]{2,1,0:T(1,128)}, u32[]{:S(2)}) copy-start(s32[1,1,130]{2,1,0:T(1,128)} %param.20) | copy-start | bytes 1564
  5.3 102.2 %copy-start.3 = (bf16[1024]{0:T(1024)(128)(2,1)S(1)}, bf16[1024]{0:T(1024)(128)(2,1)}, u32[]{:S(2)}) copy-start(bf16[1024]{0:T(1024)(128)(2,1)} %param.24) | copy-start | bytes 6148
  5.3 102.2 %copy-start.4 = (bf16[1024]{0:T(1024)(128)(2,1)S(1)}, bf16[1024]{0:T(1024)(128)(2,1)}, u32[]{:S(2)}) copy-start(bf16[1024]{0:T(1024)(128)(2,1)} %param.25) | copy-start | bytes 6148
  5.3 102.2 %copy-start.5 = (bf16[1024]{0:T(1024)(128)(2,1)S(1)}, bf16[1024]{0:T(1024)(128)(2,1)}, u32[]{:S(2)}) copy-start(bf16[1024]{0:T(1024)(128)(2,1)} %param.26) | copy-start | bytes 6148
  5.3 102.3 %copy-start.6 = (bf16[1024]{0:T(1024)(128)(2,1)S(1)}, bf16[1024]{0:T(1024)(128)(2,1)}, u32[]{:S(2)}) copy-start(bf16[1024]{0:T(1024)(128)(2,1)} %param.27) | copy-start | bytes 6148

commit v2 on v1

--- a/solution.py
+++ b/solution.py
@@ -12,10 +12,11 @@
 HEAD_ROWS = 128
 LANES = 128
 SUB = 8
-ID_PAD = 256
+K_TILE = 256
 CAP = 24
-PIECE = 256
+PIECE = 512
 MLP_BLOCK = 1024
+E_GATE = 5
 VMEM_LIMIT = 66_900_000
 F32 = jnp.float32
 BF16 = jnp.bfloat16
@@ -36,12 +37,13 @@
 
 def mega_kernel(
     n_dp, n_pp, seq, cap,
-    ids_ref, gains_ref, emb, w1h, w2h, wph, u1h, u2h, woh,
-    main_out, mtp_out, loss_out, flag_out,
+    ids_ref, gf_ref, gh_ref, ge_ref, gm_ref, emb, w1h, w2h, wph, u1h, u2h, woh,
+    out_ref, flag_out,
     w1, w2, u1, u2, wp, wo,
     ids_all, send_rows, recv_rows, xbuf, ybuf, xnb, hid, ebuf, hbuf, eall, zbuf, epart, xh, lg, mx, sm, pk,
-    part_send, part_recv, ls_send, ls_recv,
+    part_send, part_recv, ls_send, ls_recv, over_buf,
     wsem, ids_ss, ids_rs, row_ss, row_rs, x_ss, x_rs, e_ss, e_rs, h_ss, h_rs, f_ss, part_ss, part_rs, ls_ss, ls_rs,
+    over_ss, over_rs, link_free,
 ):
     d = lax.axis_index("dp")
     p = lax.axis_index("pp")
@@ -59,8 +61,10 @@
     n_piece = width // PIECE
     is_first = p == 0
     is_last = p == n_pp - 1
-    k_main = n_rows // ID_PAD * ID_PAD
-    k_pad = k_main + ID_PAD
+    k_main = n_rows // K_TILE * K_TILE
+    k_pad = k_main + K_TILE
+    n_id = seq + 2
+    n_slots = n_dp * cap
 
     col0 = pl.multiple_of(shard * (base_tiles * LANES), LANES)
     tab_cp = pltpu.make_async_copy(emb.at[0], u2.at[pl.ds(0, n_rows), :], wsem.at[0])
@@ -90,12 +94,14 @@
 
     def ids_copy(owner, peer):
         return pltpu.make_async_remote_copy(
-            src_ref=ids_ref, dst_ref=ids_all.at[owner], send_sem=ids_ss.at[peer], recv_sem=ids_rs.at[owner],
+            src_ref=ids_ref.at[0], dst_ref=ids_all.at[owner], send_sem=ids_ss.at[peer], recv_sem=ids_rs.at[owner],
             device_id={"dp": peer}, device_id_type=MESH)
 
-    for k in range(1, n_dp):
-        ids_copy(d, lax.rem(d + k, n_dp)).start()
-    ids_all[d] = ids_ref[...]
+    @pl.when(is_first)
+    def _():
+        for k in range(1, n_dp):
+            ids_copy(d, lax.rem(d + k, n_dp)).start()
+        ids_all[d] = ids_ref[0]
 
     @pl.when(jnp.logical_not(is_first))
     def _():
@@ -104,53 +110,59 @@
         wp_cp.start()
         wo_cp.start()
 
-    for k in range(1, n_dp):
-        peer = lax.rem(d + k, n_dp)
-        ids_copy(peer, peer).wait_recv()
-
-    def set_flag():
-        ids2 = ids_all[...].reshape(n_dp * SUB, ID_PAD)
-        used = iota((n_dp * SUB, ID_PAD), 1) < seq + 1
-        most = jnp.zeros((n_dp * SUB, 1), F32)
-        for k in range(n_dp):
-            hit = (ids2 >= k * n_rows) & (ids2 < (k + 1) * n_rows) & used
-            most = jnp.maximum(most, jnp.sum(jnp.where(hit, 1.0, 0.0), axis=1, keepdims=True))
-        over = jnp.max(most, axis=0, keepdims=True)
-        flag_out[...] = jnp.broadcast_to(jnp.where(over > cap, 1.0, 0.0), (SUB, LANES))
-
     def row_copy(owner, peer):
         return pltpu.make_async_remote_copy(
             src_ref=send_rows.at[peer], dst_ref=recv_rows.at[owner], send_sem=row_ss.at[peer], recv_sem=row_rs.at[owner],
             device_id={"dp": peer}, device_id_type=MESH)
 
+    def positions(row0, n):
+        row = ids_ref[0]
+        rr = iota((n, n_id), 0) + row0
+        ll = iota((n, n_id), 1)
+        pos = jnp.where(rr < seq, rr, rr - seq + 1)
+        id_col = jnp.sum(jnp.where(ll == pos, jnp.broadcast_to(row, (n, n_id)), 0).astype(F32), axis=1, keepdims=True)
+        src_col = jnp.zeros((n, 1), F32)
+        src_row = jnp.zeros((1, n_id), F32)
+        for k in range(1, n_dp):
+            src_col = src_col + jnp.where(id_col >= float(k * n_rows), 1.0, 0.0)
+            src_row = src_row + jnp.where(row >= k * n_rows, 1.0, 0.0)
+        earlier = (jnp.broadcast_to(src_row, (n, n_id)) == src_col) & (ll < pos)
+        rank_col = jnp.sum(jnp.where(earlier, 1.0, 0.0), axis=1, keepdims=True)
+        where_col = jnp.where(rank_col < float(cap), src_col * float(cap) + rank_col, -1.0).astype(jnp.int32)
+        return jnp.where(iota((n, n_slots), 1) == where_col, 1.0, 0.0).astype(BF16)
+
     @pl.when(is_first)
     def _():
+        xnb[:, 0:n_slots] = positions(0, seq)
+        eall[:, 0:n_slots] = positions(seq, seq)
+        for k in range(1, n_dp):
+            peer = lax.rem(d + k, n_dp)
+            ids_copy(peer, peer).wait_recv()
         w1_cp.start()
         w2_cp.start()
         low = d * n_rows
-        ids2 = ids_all[...].reshape(n_dp * SUB, ID_PAD)
-        lane2 = iota((n_dp * SUB, ID_PAD), 1)
+        ids2 = ids_all[...].reshape(n_dp, n_id)
+        lane2 = iota((n_dp, n_id), 1)
         valid = (ids2 >= low) & (ids2 < low + n_rows) & (lane2 < seq + 1)
-        before = jnp.where(iota((ID_PAD, ID_PAD), 0) < iota((ID_PAD, ID_PAD), 1), 1.0, 0.0).astype(BF16)
+        before = jnp.where(iota((n_id, n_id), 0) < iota((n_id, n_id), 1), 1.0, 0.0).astype(BF16)
         rank = dot32(jnp.where(valid, 1.0, 0.0).astype(BF16), before)
         key = jnp.where(valid, rank, -1.0)
         loc = jnp.where(valid, ids2 - low, 0).astype(F32)
-        slot = iota((cap, ID_PAD), 0).astype(F32)
+        slot = iota((cap, n_id), 0).astype(F32)
         for b in range(0, n_dp, 2):
             picks = []
             for s in (b, b + 1):
-                sel = key[s * SUB:s * SUB + 1, :] == slot
-                idx = jnp.sum(jnp.where(sel, loc[s * SUB:s * SUB + 1, :] + 1.0, 0.0), axis=1, keepdims=True) - 1.0
+                sel = key[s:s + 1, :] == slot
+                idx = jnp.sum(jnp.where(sel, loc[s:s + 1, :] + 1.0, 0.0), axis=1, keepdims=True) - 1.0
                 picks.append(idx)
             idx2 = jnp.concatenate(picks, axis=0).astype(jnp.int32)
             hot = jnp.where(iota((2 * cap, k_pad), 1) == idx2, 1.0, 0.0).astype(BF16)
             u1[b * cap:(b + 2) * cap, 0:k_pad] = hot
         tab_cp.wait()
-        n_slots = n_dp * cap
         blk = min(512, width)
         for c in range(0, width, blk):
             tail = u2[k_main:k_pad, c:c + blk]
-            tail = jnp.where(iota((ID_PAD, blk), 0) < n_rows - k_main, tail.astype(F32), 0.0).astype(BF16)
+            tail = jnp.where(iota((K_TILE, blk), 0) < n_rows - k_main, tail.astype(F32), 0.0).astype(BF16)
             got = dot32(u1[0:n_slots, 0:k_main], u2[0:k_main, c:c + blk]) + dot32(u1[0:n_slots, k_main:k_pad], tail)
             for s in range(n_dp):
                 send_rows[s, :, c:c + blk] = got[s * cap:(s + 1) * cap, :].astype(BF16)
@@ -161,30 +173,10 @@
         u2_cp.start()
         wp_cp.start()
         wo_cp.start()
-        row = ids_ref[0:1, :]
-        rr = iota((2 * seq, ID_PAD), 0)
-        ll = iota((2 * seq, ID_PAD), 1)
-        pos = jnp.where(rr < seq, rr, rr - seq + 1)
-        id_col = jnp.sum(jnp.where(ll == pos, jnp.broadcast_to(row, (2 * seq, ID_PAD)), 0).astype(F32), axis=1, keepdims=True)
-        src_col = jnp.zeros((2 * seq, 1), F32)
-        src_row = jnp.zeros((1, ID_PAD), F32)
-        for k in range(1, n_dp):
-            src_col = src_col + jnp.where(id_col >= float(k * n_rows), 1.0, 0.0)
-            src_row = src_row + jnp.where(row >= k * n_rows, 1.0, 0.0)
-        earlier = (jnp.broadcast_to(src_row, (2 * seq, ID_PAD)) == src_col) & (ll < pos)
-        rank_col = jnp.sum(jnp.where(earlier, 1.0, 0.0), axis=1, keepdims=True)
-        where_col = jnp.where(rank_col < float(cap), src_col * float(cap) + rank_col, -1.0).astype(jnp.int32)
-        place = jnp.where(iota((2 * seq, n_slots), 1) == where_col, 1.0, 0.0).astype(BF16)
         for k in range(1, n_dp):
             peer = lax.rem(d + k, n_dp)
             row_copy(peer, peer).wait_recv()
-        rows = dot32(place, recv_rows[...].reshape(n_slots, width)).astype(BF16)
-        xbuf[...] = rows[0:seq, :]
-        eall[...] = rows[seq:2 * seq, :]
-
-    @pl.when(jnp.logical_not(is_first))
-    def _():
-        set_flag()
+        xbuf[...] = dot32(xnb[:, 0:n_slots], recv_rows[...].reshape(n_slots, width)).astype(BF16)
 
     def x_copy(i):
         part = pl.ds(i * PIECE, PIECE)
@@ -212,15 +204,19 @@
             hid[0:m, c:c + MLP_BLOCK] = jax.nn.gelu(dot32(xn, w_up[:, c:c + MLP_BLOCK])).astype(BF16)
 
     w1_cp.wait()
+    w2_cp.wait()
 
     @pl.when(jnp.logical_not(is_first))
     def _():
         for i in range(n_piece):
             x_copy(i).wait_recv()
 
+    @pl.when(p == E_GATE)
+    def _():
+        pl.semaphore_signal(link_free, inc=1, device_id={"pp": 0}, device_id_type=MESH)
+
     xnb[...] = norm_f32(xbuf[...].astype(F32)).astype(BF16)
     gelu_up(seq, xnb[...], w1)
-    w2_cp.wait()
     for i in range(n_piece):
         c = i * PIECE
         out = xbuf[:, c:c + PIECE].astype(F32) + dot32(hid[...], w2[:, c:c + PIECE])
@@ -243,21 +239,35 @@
             src_ref=eall.at[pl.ds(row0, half), :], dst_ref=ebuf, send_sem=e_ss.at[to], recv_sem=e_rs,
             device_id={"pp": to}, device_id_type=MESH)
 
+    def over_copy(to):
+        return pltpu.make_async_remote_copy(
+            src_ref=over_buf.at[0], dst_ref=over_buf.at[1], send_sem=over_ss.at[to], recv_sem=over_rs,
+            device_id={"pp": to}, device_id_type=MESH)
+
     @pl.when(is_first)
     def _():
+        eall[...] = dot32(eall[:, 0:n_slots], recv_rows[...].reshape(n_slots, width)).astype(BF16)
+        ids2 = ids_all[...].reshape(n_dp, n_id)
+        used = iota((n_dp, n_id), 1) < seq + 1
+        most = jnp.zeros((n_dp, 1), F32)
+        for k in range(n_dp):
+            hit = (ids2 >= k * n_rows) & (ids2 < (k + 1) * n_rows) & used
+            most = jnp.maximum(most, jnp.sum(jnp.where(hit, 1.0, 0.0), axis=1, keepdims=True))
+        over = jnp.broadcast_to(jnp.where(jnp.max(most, axis=0, keepdims=True) > cap, 1.0, 0.0), (SUB, LANES))
+        over_buf[0] = over
+        over_buf[1] = over
+        ebuf[...] = eall[0:half, :]
+        pl.semaphore_wait(link_free, 1)
         for to in range(1, n_pp):
             e_copy(to).start()
-        ebuf[...] = eall[0:half, :]
-        set_flag()
+            over_copy(to).start()
 
     @pl.when(jnp.logical_not(is_first))
     def _():
         e_copy(1).wait_recv()
-
-    g_f = gains_ref[0:1, :]
-    g_h = gains_ref[1:2, :]
-    g_e = gains_ref[2:3, :]
-    g_m = gains_ref[3:4, :]
+        over_copy(1).wait_recv()
+
+    g_f, g_h, g_e, g_m = (ref[...].astype(F32).reshape(1, width) for ref in (gf_ref, gh_ref, ge_ref, gm_ref))
 
     wp_cp.wait()
     e_n = (norm_f32(ebuf[...].astype(F32)) * g_e).astype(BF16)
@@ -266,10 +276,10 @@
     u2_cp.wait()
     wo_cp.wait()
 
-    row_f = jnp.broadcast_to(ids_ref[0:1, :], (2 * half, ID_PAD))
-    rr = iota((2 * half, ID_PAD), 0)
+    row_f = jnp.broadcast_to(ids_ref[0], (2 * half, n_id))
+    rr = iota((2 * half, n_id), 0)
     at = jnp.where(rr < half, rr + 1, rr - half + 2) + group * half
-    tgt = jnp.sum(jnp.where(iota((2 * half, ID_PAD), 1) == at, row_f, 0).astype(F32), axis=1, keepdims=True)
+    tgt = jnp.sum(jnp.where(iota((2 * half, n_id), 1) == at, row_f, 0).astype(F32), axis=1, keepdims=True)
     tgt = tgt.astype(jnp.int32) - shard * (base_tiles * LANES)
     tgt = jnp.broadcast_to(tgt, (2 * half, LANES))
 
@@ -372,8 +382,6 @@
     low_lane = iota((SUB, LANES), 1) < half
     main = jnp.where(low_lane, nll_a, pltpu.roll(nll_b, half, 1))
     mtp = jnp.where(low_lane, pltpu.roll(nll_a, half, 1), nll_b)
-    main_out[...] = main[0:1, :]
-    mtp_out[...] = mtp[0:1, :]
     both = main + MTP_WEIGHT * mtp
     ls_send[...] = both
     ls_recv[d] = both
@@ -391,21 +399,23 @@
     acc = ls_recv[0]
     for k in range(1, n_dp):
         acc = acc + ls_recv[k]
-    loss_out[...] = jnp.broadcast_to(jnp.sum(acc, axis=1, keepdims=True) * (1.0 / (n_dp * seq)), (SUB, LANES))
+    loss = jnp.sum(acc, axis=1, keepdims=True) * (1.0 / (n_dp * seq))
+    out_ref[...] = jnp.where(sub == 0, main, jnp.where(sub == 1, mtp, jnp.broadcast_to(loss, (SUB, LANES))))
+    flag_out[0, 0] = jnp.max(over_buf[1]).astype(jnp.int32)
 
     for k in range(1, n_dp):
-        peer = lax.rem(d + k, n_dp)
-        ids_copy(d, peer).wait_send()
-        ls_copy(d, peer).wait_send()
+        ls_copy(d, lax.rem(d + k, n_dp)).wait_send()
     for k in range(1, n_pp):
         part_copy(p, lax.rem(p + k, n_pp)).wait_send()
 
     @pl.when(is_first)
     def _():
         for k in range(1, n_dp):
+            ids_copy(d, lax.rem(d + k, n_dp)).wait_send()
             row_copy(d, lax.rem(d + k, n_dp)).wait_send()
         for to in range(1, n_pp):
             e_copy(to).wait_send()
+            over_copy(to).wait_send()
 
     @pl.when(jnp.logical_not(is_last))
     def _():
@@ -440,13 +450,11 @@
     return pl.pallas_call(
         functools.partial(mega_kernel, n_dp, n_pp, seq, CAP),
         out_shape=(
-            jax.ShapeDtypeStruct((1, seq), F32),
-            jax.ShapeDtypeStruct((1, seq), F32),
             jax.ShapeDtypeStruct((SUB, LANES), F32),
-            jax.ShapeDtypeStruct((SUB, LANES), F32),
+            jax.ShapeDtypeStruct((1, 1), jnp.int32),
         ),
-        in_specs=[vmem] * 2 + [anys] * 7,
-        out_specs=(vmem,) * 4,
+        in_specs=[vmem] * 5 + [anys] * 7,
+        out_specs=(vmem, pl.BlockSpec(memory_space=pltpu.SMEM)),
         scratch_shapes=[
             pltpu.VMEM((width, ffn), BF16),
             pltpu.VMEM((ffn, width), BF16),
@@ -454,7 +462,7 @@
             pltpu.VMEM((ffn, width), BF16),
             pltpu.VMEM((2 * width, width), BF16),
             pltpu.VMEM((width, cols - ffn), BF16),
-            pltpu.VMEM((n_dp, SUB, ID_PAD), jnp.int32),
+            pltpu.VMEM((n_dp, 1, seq + 2), jnp.int32),
             pltpu.VMEM((n_dp, CAP, width), BF16),
             pltpu.VMEM((n_dp, CAP, width), BF16),
             act, act, act,
@@ -468,13 +476,14 @@
             pltpu.VMEM((2 * half, LANES), F32), pltpu.VMEM((2 * half, LANES), F32), pltpu.VMEM((2 * half, LANES), F32),
             tile, pltpu.VMEM((n_pp, SUB, LANES), F32),
             tile, pltpu.VMEM((n_dp, SUB, LANES), F32),
+            pltpu.VMEM((2, SUB, LANES), F32),
             dma((8,)), dma((n_dp,)), dma((n_dp,)), dma((n_dp,)), dma((n_dp,)),
             dma((n_piece,)), dma((n_piece,)), dma((n_pp,)), dma(()), dma((4, n_piece)), dma((n_piece,)), dma((n_piece,)),
-            dma((n_pp,)), dma((n_pp,)), dma((n_dp,)), dma((n_dp,)),
+            dma((n_pp,)), dma((n_pp,)), dma((n_dp,)), dma((n_dp,)), dma((n_pp,)), dma(()), pltpu.SemaphoreType.REGULAR,
         ],
         compiler_params=pltpu.CompilerParams(collective_id=0, has_side_effects=True, vmem_limit_bytes=VMEM_LIMIT),
         name="mtp_eval",
-    )(ids, gains, emb, w1, w2, wp, u1, u2, wo)
+    )(ids, *gains, emb, w1, w2, wp, u1, u2, wo)
 
 
 def norm_plain(x_val):
@@ -552,20 +561,16 @@
 
     def body(tok_ids, emb_s, w_one, w_two, gain_f, gain_h, gain_e, gain_m, w_proj, u_one, u_two, w_out):
         seq = tok_ids.shape[2] - 2
-        ids = tok_ids.reshape(1, seq + 2)
-        ids_pad = jnp.pad(jnp.broadcast_to(ids, (SUB, seq + 2)), ((0, 0), (0, ID_PAD - seq - 2)), constant_values=-1)
-        gains = jnp.stack([gain_f, gain_h, gain_e, gain_m] * 2).astype(F32)
-        main_nll, mtp_nll, total, over = mega(n_dp, n_pp, seq, ids_pad, gains, emb_s, w_one, w_two, w_proj, u_one, u_two, w_out)
+        gains = (gain_f, gain_h, gain_e, gain_m)
+        packed, over = mega(n_dp, n_pp, seq, tok_ids, gains, emb_s, w_one, w_two, w_proj, u_one, u_two, w_out)
 
         def slow():
-            return any_ids(n_dp, n_pp, seq, ids[0], emb_s[0], w_one[0, 0], w_two[0, 0], gain_f, gain_h, gain_e, gain_m,
-                           w_proj, u_one, u_two, w_out)
-
-        def fast():
-            return total[0, 0], main_nll, mtp_nll
-
-        loss, main_nll, mtp_nll = lax.cond(over[0, 0] > 0.0, slow, fast)
-        return loss, main_nll.reshape(1, 1, seq), mtp_nll.reshape(1, 1, seq)
+            total, main_nll, mtp_nll = any_ids(
+                n_dp, n_pp, seq, tok_ids[0, 0], emb_s[0], w_one[0, 0], w_two[0, 0], *gains, w_proj, u_one, u_two, w_out)
+            return jnp.concatenate([main_nll, mtp_nll, jnp.broadcast_to(total, (SUB - 2, seq))], axis=0)
+
+        packed = lax.cond(over[0, 0] > 0, slow, lambda: packed)
+        return packed[2, 0], packed[0:1].reshape(1, 1, seq), packed[1:2].reshape(1, 1, seq)
 
     rep = P()
     in_specs = (P(None, "dp", None), P("pp", "dp", None), P("pp"), P("pp"), rep, rep, rep, rep, rep, rep, rep, rep)

time: 111 us -> 95 us (0.86)
  Pallas kernels: 100 us -> 90.6 us
  local copies, waits for them, and re-layouts: 8.05 us -> 2.47 us
    pallas_call x1, Pallas kernels: 100 us -> 90.6 us  [mega(): pl.pallas_call(functools.partial(mega_kernel, n_dp, n_pp, seq, CAP), out_...]
    another operation x5 -> x0, local copies, waits for them, and re-layouts: 2.8 us -> none  [body(): gains = jnp.stack([gain_f, gain_h, gain_e, gain_m] * 2).astype(F32)]
    unnamed x12 -> x10, local copies, waits for them, and re-layouts: 2.27 us -> 0.02 us
    pad x2 -> x0, local copies, waits for them, and re-layouts: 1.28 us -> none  [body(): jnp.pad(jnp.broadcast_to(ids, (SUB, seq + 2)), ((0, 0), (0, ID_PAD - seq...]
    reshape x0 -> x1, local copies, waits for them, and re-layouts: none -> 1.27 us  [body(): packed[1:2].reshape(1, 1, seq)]
where the time goes in v2:
time: 95 us; the launch traced here: 94.7 us
  Pallas kernels  90.6 us (95%)
  local copies, waits for them, and re-layouts  2.47 us (3%)
  between operations  1.42 us (1%)
    pallas_call x1, Pallas kernels, mega(): pl.pallas_call(functools.partial(mega_kernel, n_dp, n_pp, seq, CAP), out_...  90.6 us

profile of v2, /device:TPU:1, one launch (start us, length us, event | category | flops | bytes accessed | tf_op | source)
XLA Modules:
  0.0 94.7 jit_solution(18287669642910033760)
XLA Ops:
  0.6 0.0 copy-start.2
  0.6 0.0 copy-start.3
  0.7 0.0 copy-start.4
  0.7 0.0 copy-start.5
  0.7 0.0 copy-start.6
  0.7 90.6 %mtp_eval.1 = (f32[8,128]{1,0:T(8,128)}, s32[1,1]{1,0:T(1,128)}) custom-call(s32[1,1,130]{2,1,0:T(1,128)} %ids_ref.1, bf16[1024]{0:T(1024)(128)(2,1)} %gf_ref.1, bf16[1024]{0:T(1024)(128)(2,1)} %gh_ref.1, bf16[1024]{0:T(1024)(128)(2,1)} %ge_ref.1, bf16[1024]{0:T(1024)(128)(2,1)} %gm_ref.1, bf16[1,3144,1024]{2,1,0:T(8,128)(2,1)} %emb.1, ...), custom_call_target="tpu_custom_call" | custom-call | tf_op jit(solution)/shard_map/mtp_eval/pallas_call | solution.py:450
  92.0 0.0 copy-done.2
  92.0 0.0 copy-done.3
  92.0 0.0 copy-done.4
  92.0 0.0 copy-done.5
  92.0 0.0 copy-done.6
  92.0 0.3 conditional.1
  92.3 1.2 %slice.41 = f32[1,1]{1,0:T(1,128)} slice(f32[8,128]{1,0:T(8,128)} %get-tuple-element.510), slice={[2:3], [0:1]} | slice | bytes 8 | tf_op jit(solution)/shard_map/slice | solution.py:573
  93.5 1.3 %slice_bitcast_fusion = (f32[1,1,128]{2,1,0:T(1,128)}, f32[1,1,128]{2,1,0:T(1,128)}) fusion(f32[8,128]{1,0:T(8,128)} %get-tuple-element.510), kind=kLoop, calls=%fused_computation.121 | loop fusion | bytes 2048 | tf_op jit(solution)/shard_map/reshape | solution.py:573
Async XLA Ops:
  0.6 91.3 %copy-start.2 = (s32[1,1,130]{2,1,0:T(1,128)S(1)}, s32[1,1,130]{2,1,0:T(1,128)}, u32[]{:S(2)}) copy-start(s32[1,1,130]{2,1,0:T(1,128)} %ids_ref.1) | copy-start | bytes 1564
  0.6 91.3 %copy-start.3 = (bf16[1024]{0:T(1024)(128)(2,1)S(1)}, bf16[1024]{0:T(1024)(128)(2,1)}, u32[]{:S(2)}) copy-start(bf16[1024]{0:T(1024)(128)(2,1)} %gf_ref.1) | copy-start | bytes 6148
  0.7 91.3 %copy-start.4 = (bf16[1024]{0:T(1024)(128)(2,1)S(1)}, bf16[1024]{0:T(1024)(128)(2,1)}, u32[]{:S(2)}) copy-start(bf16[1024]{0:T(1024)(128)(2,1)} %gh_ref.1) | copy-start | bytes 6148
  0.7 91.3 %copy-start.5 = (bf16[1024]{0:T(1024)(128)(2,1)S(1)}, bf16[1024]{0:T(1024)(128)(2,1)}, u32[]{:S(2)}) copy-start(bf16[1024]{0:T(1024)(128)(2,1)} %ge_ref.1) | copy-start | bytes 6148
  0.7 91.3 %copy-start.6 = (bf16[1024]{0:T(1024)(128)(2,1)S(1)}, bf16[1024]{0:T(1024)(128)(2,1)}, u32[]{:S(2)}) copy-start(bf16[1024]{0:T(1024)(128)(2,1)} %gm_ref.1) | copy-start | bytes 6148

commit v3 on v2

--- a/solution.py
+++ b/solution.py
@@ -39,16 +39,16 @@
     n_dp, n_pp, seq, cap,
     ids_ref, gf_ref, gh_ref, ge_ref, gm_ref, emb, w1h, w2h, wph, u1h, u2h, woh,
     out_ref, flag_out,
-    w1, w2, u1, u2, wp, wo,
+    w1, w2, wp, wo,
     ids_all, send_rows, recv_rows, xbuf, ybuf, xnb, hid, ebuf, hbuf, eall, zbuf, epart, xh, lg, mx, sm, pk,
     part_send, part_recv, ls_send, ls_recv, over_buf,
     wsem, ids_ss, ids_rs, row_ss, row_rs, x_ss, x_rs, e_ss, e_rs, h_ss, h_rs, f_ss, part_ss, part_rs, ls_ss, ls_rs,
-    over_ss, over_rs, link_free,
+    over_ss, over_rs, link_free, push_ss, push_rs,
 ):
     d = lax.axis_index("dp")
     p = lax.axis_index("pp")
     width = xbuf.shape[1]
-    ffn = w1.shape[1]
+    ffn = w1.shape[2]
     n_rows = emb.shape[1]
     half = seq // 2
     n_shard = n_pp // 2
@@ -56,31 +56,40 @@
     group = p // n_shard
     n_tiles = woh.shape[1] // LANES
     base_tiles = n_tiles // n_shard
-    cols = w1.shape[1] + wo.shape[1]
+    cols = ffn + wo.shape[1]
     own_cols = wo.shape[1]
     n_piece = width // PIECE
     is_first = p == 0
     is_last = p == n_pp - 1
+    even = lax.rem(p, 2) == 0
+    lender = even & (p > 1)
+    double = jnp.logical_not(even) & (p > 1)
     k_main = n_rows // K_TILE * K_TILE
     k_pad = k_main + K_TILE
     n_id = seq + 2
     n_slots = n_dp * cap
 
     col0 = pl.multiple_of(shard * (base_tiles * LANES), LANES)
-    tab_cp = pltpu.make_async_copy(emb.at[0], u2.at[pl.ds(0, n_rows), :], wsem.at[0])
-    w1_cp = pltpu.make_async_copy(w1h.at[0, 0], w1, wsem.at[1])
-    w2_cp = pltpu.make_async_copy(w2h.at[0, 0], w2, wsem.at[2])
-    u1_cp = pltpu.make_async_copy(u1h, u1, wsem.at[3])
-    u2_cp = pltpu.make_async_copy(u2h, u2, wsem.at[4])
+    tab_cp = pltpu.make_async_copy(emb.at[0], w2.at[0, pl.ds(0, n_rows), :], wsem.at[0])
+    w1_cp = pltpu.make_async_copy(w1h.at[0, 0], w1.at[1], wsem.at[1])
+    w2_cp = pltpu.make_async_copy(w2h.at[0, 0], w2.at[1], wsem.at[2])
+    u1_cp = pltpu.make_async_copy(u1h, w1.at[0], wsem.at[3])
+    u2_cp = pltpu.make_async_copy(u2h, w2.at[0], wsem.at[4])
     wp_cp = pltpu.make_async_copy(wph, wp, wsem.at[5])
     wo_cp = pltpu.make_async_copy(woh.at[:, pl.ds(col0 + ffn, own_cols)], wo, wsem.at[6])
-    late_cp = pltpu.make_async_copy(woh.at[:, pl.ds(col0, ffn)], w1, wsem.at[7])
+    late_cp = pltpu.make_async_copy(woh.at[:, pl.ds(col0, ffn)], w1.at[1], wsem.at[7])
+
+    def push_copy(i):
+        src, dst = ((w1h, w1), (w2h, w2))[i]
+        return pltpu.make_async_remote_copy(
+            src_ref=src.at[0, 0], dst_ref=dst.at[0], send_sem=push_ss.at[i], recv_sem=push_rs.at[i],
+            device_id={"pp": lax.rem(p + 1, n_pp)}, device_id_type=MESH)
 
     @pl.when(is_first)
     def _():
         tab_cp.start()
 
-    @pl.when(jnp.logical_not(is_first))
+    @pl.when(jnp.logical_not(even))
     def _():
         w1_cp.start()
         w2_cp.start()
@@ -103,17 +112,34 @@
             ids_copy(d, lax.rem(d + k, n_dp)).start()
         ids_all[d] = ids_ref[0]
 
-    @pl.when(jnp.logical_not(is_first))
-    def _():
+    @pl.when(lender)
+    def _():
+        push_copy(0).start()
+        push_copy(1).start()
         u1_cp.start()
         u2_cp.start()
+        late_cp.start()
+
+    @pl.when(p == 1)
+    def _():
+        u1_cp.start()
+        u2_cp.start()
+
+    @pl.when(jnp.logical_not(is_first))
+    def _():
         wp_cp.start()
         wo_cp.start()
 
-    def row_copy(owner, peer):
-        return pltpu.make_async_remote_copy(
-            src_ref=send_rows.at[peer], dst_ref=recv_rows.at[owner], send_sem=row_ss.at[peer], recv_sem=row_rs.at[owner],
-            device_id={"dp": peer}, device_id_type=MESH)
+    n_y = 4
+    n_z = n_dp // n_y
+    offs = [(z, y) for z in range(n_z) for y in range(n_y)]
+    offs.sort(key=lambda o: -(min(o[0], n_z - o[0]) + min(o[1], n_y - o[1])))
+    order = [lax.rem(d // n_y + z, n_z) * n_y + lax.rem(d + y, n_y) for z, y in offs]
+
+    def row_copy(owner, j):
+        return pltpu.make_async_remote_copy(
+            src_ref=send_rows.at[j], dst_ref=recv_rows.at[owner], send_sem=row_ss.at[j], recv_sem=row_rs.at[owner],
+            device_id={"dp": order[j]}, device_id_type=MESH)
 
     def positions(row0, n):
         row = ids_ref[0]
@@ -141,7 +167,7 @@
         w1_cp.start()
         w2_cp.start()
         low = d * n_rows
-        ids2 = ids_all[...].reshape(n_dp, n_id)
+        ids2 = jnp.concatenate([ids_all[peer] for peer in order], axis=0)
         lane2 = iota((n_dp, n_id), 1)
         valid = (ids2 >= low) & (ids2 < low + n_rows) & (lane2 < seq + 1)
         before = jnp.where(iota((n_id, n_id), 0) < iota((n_id, n_id), 1), 1.0, 0.0).astype(BF16)
@@ -157,34 +183,36 @@
                 picks.append(idx)
             idx2 = jnp.concatenate(picks, axis=0).astype(jnp.int32)
             hot = jnp.where(iota((2 * cap, k_pad), 1) == idx2, 1.0, 0.0).astype(BF16)
-            u1[b * cap:(b + 2) * cap, 0:k_pad] = hot
+            w1[0, b * cap:(b + 2) * cap, 0:k_pad] = hot
         tab_cp.wait()
         blk = min(512, width)
-        for c in range(0, width, blk):
-            tail = u2[k_main:k_pad, c:c + blk]
-            tail = jnp.where(iota((K_TILE, blk), 0) < n_rows - k_main, tail.astype(F32), 0.0).astype(BF16)
-            got = dot32(u1[0:n_slots, 0:k_main], u2[0:k_main, c:c + blk]) + dot32(u1[0:n_slots, k_main:k_pad], tail)
-            for s in range(n_dp):
-                send_rows[s, :, c:c + blk] = got[s * cap:(s + 1) * cap, :].astype(BF16)
-        for k in range(1, n_dp):
-            row_copy(d, lax.rem(d + k, n_dp)).start()
-        recv_rows[d] = send_rows[d]
+        n_half = n_dp // 2
+        for h in range(2):
+            r0, r1 = h * n_half * cap, (h + 1) * n_half * cap
+            for c in range(0, width, blk):
+                tail = w2[0, k_main:k_pad, c:c + blk]
+                tail = jnp.where(iota((K_TILE, blk), 0) < n_rows - k_main, tail.astype(F32), 0.0).astype(BF16)
+                got = dot32(w1[0, r0:r1, 0:k_main], w2[0, 0:k_main, c:c + blk]) + dot32(w1[0, r0:r1, k_main:k_pad], tail)
+                for s in range(n_half):
+                    send_rows[h * n_half + s, :, c:c + blk] = got[s * cap:(s + 1) * cap, :].astype(BF16)
+            for j in range(h * n_half, min((h + 1) * n_half, n_dp - 1)):
+                row_copy(d, j).start()
+        recv_rows[d] = send_rows[n_dp - 1]
         u1_cp.start()
         u2_cp.start()
         wp_cp.start()
         wo_cp.start()
-        for k in range(1, n_dp):
-            peer = lax.rem(d + k, n_dp)
-            row_copy(peer, peer).wait_recv()
+        for j in range(n_dp - 1):
+            row_copy(order[j], j).wait_recv()
         xbuf[...] = dot32(xnb[:, 0:n_slots], recv_rows[...].reshape(n_slots, width)).astype(BF16)
 
     def x_copy(i):
         part = pl.ds(i * PIECE, PIECE)
         return pltpu.make_async_remote_copy(
             src_ref=ybuf.at[:, part], dst_ref=xbuf.at[:, part], send_sem=x_ss.at[i], recv_sem=x_rs.at[i],
-            device_id={"pp": lax.rem(p + 1, n_pp)}, device_id_type=MESH)
-
-    h_peers = ((1, 0), (3, 0), (5, half), (6, half))
+            device_id={"pp": jnp.where(is_first, 1, lax.rem(p + 2, n_pp))}, device_id_type=MESH)
+
+    h_peers = ((3, 0), (1, 0), (5, half), (6, half))
 
     def h_copy(j, i):
         to, row0 = h_peers[j]
@@ -199,39 +227,63 @@
             src_ref=hbuf.at[:, part], dst_ref=hbuf.at[:, part], send_sem=f_ss.at[i], recv_sem=h_rs.at[i],
             device_id={"pp": lax.rem(p + n_pp - 1, n_pp)}, device_id_type=MESH)
 
-    def gelu_up(m, xn, w_up):
+    def gelu_up(m, xn, slot):
         for c in range(0, ffn, MLP_BLOCK):
-            hid[0:m, c:c + MLP_BLOCK] = jax.nn.gelu(dot32(xn, w_up[:, c:c + MLP_BLOCK])).astype(BF16)
-
-    w1_cp.wait()
-    w2_cp.wait()
-
-    @pl.when(jnp.logical_not(is_first))
-    def _():
-        for i in range(n_piece):
-            x_copy(i).wait_recv()
-
-    @pl.when(p == E_GATE)
-    def _():
-        pl.semaphore_signal(link_free, inc=1, device_id={"pp": 0}, device_id_type=MESH)
-
-    xnb[...] = norm_f32(xbuf[...].astype(F32)).astype(BF16)
-    gelu_up(seq, xnb[...], w1)
-    for i in range(n_piece):
-        c = i * PIECE
-        out = xbuf[:, c:c + PIECE].astype(F32) + dot32(hid[...], w2[:, c:c + PIECE])
-        ybuf[:, c:c + PIECE] = out.astype(BF16)
-
-        @pl.when(jnp.logical_not(is_last))
+            hid[0:m, c:c + MLP_BLOCK] = jax.nn.gelu(dot32(xn, w1[slot, :, c:c + MLP_BLOCK])).astype(BF16)
+
+    def stage(turn, carry):
+        lent = turn == 0
+
+        @pl.when(jnp.where(lent, double, jnp.logical_not(lender)))
         def _():
-            x_copy(i).start()
-
-        @pl.when(is_last)
-        def _():
-            for j in range(len(h_peers)):
-                h_copy(j, i).start()
-
-    late_cp.start()
+            @pl.when(lent)
+            def _():
+                push_copy(0).wait_recv()
+                push_copy(1).wait_recv()
+
+            @pl.when(jnp.logical_not(lent))
+            def _():
+                w1_cp.wait()
+                w2_cp.wait()
+
+            @pl.when(lent | (p == 1))
+            def _():
+                for i in range(n_piece):
+                    x_copy(i).wait_recv()
+
+            @pl.when(lent & (p == E_GATE))
+            def _():
+                pl.semaphore_signal(link_free, inc=1, device_id={"pp": 0}, device_id_type=MESH)
+
+            xnb[...] = norm_f32(xbuf[...].astype(F32)).astype(BF16)
+            gelu_up(seq, xnb[...], turn)
+            for i in range(n_piece):
+                c = i * PIECE
+                out = xbuf[:, c:c + PIECE].astype(F32) + dot32(hid[...], w2[turn, :, c:c + PIECE])
+                ybuf[:, c:c + PIECE] = out.astype(BF16)
+
+                @pl.when(jnp.logical_not(lent | is_last))
+                def _():
+                    x_copy(i).start()
+
+                @pl.when(jnp.logical_not(lent) & is_last)
+                def _():
+                    for j in range(len(h_peers)):
+                        h_copy(j, i).start()
+
+            @pl.when(lent)
+            def _():
+                u1_cp.start()
+                u2_cp.start()
+                xbuf[...] = ybuf[...]
+
+            @pl.when(jnp.logical_not(lent))
+            def _():
+                late_cp.start()
+
+        return carry
+
+    lax.fori_loop(0, 2, stage, 0)
 
     def e_copy(to):
         row0 = half * (to // n_shard)
@@ -301,14 +353,14 @@
     zbuf[...] = z_val
     xh[0:half, :] = (h_f * g_f).astype(BF16)
     xnb[0:half, :] = (norm_f32(z_val.astype(F32)) * g_m).astype(BF16)
-    gelu_up(half, xnb[0:half, :], u1)
-    z_out = (zbuf[...].astype(F32) + dot32(hid[0:half, :], u2[...])).astype(BF16)
+    gelu_up(half, xnb[0:half, :], 0)
+    z_out = (zbuf[...].astype(F32) + dot32(hid[0:half, :], w2[0])).astype(BF16)
     xh[half:2 * half, :] = (norm_f32(z_out.astype(F32)) * g_f).astype(BF16)
 
     lane = iota((2 * half, LANES), 1)
     tail_ok = jnp.broadcast_to(shard == n_shard - 1, (2 * half, LANES))
     blocks = [(wo, c, ffn + c, min(MLP_BLOCK, own_cols - c)) for c in range(0, own_cols, MLP_BLOCK)]
-    blocks += [(w1, c, c, MLP_BLOCK) for c in range(0, ffn, MLP_BLOCK)]
+    blocks += [(w1.at[1], c, c, MLP_BLOCK) for c in range(0, ffn, MLP_BLOCK)]
 
     def logits_of(i):
         ref, c, _, n = blocks[i]
@@ -412,15 +464,21 @@
     def _():
         for k in range(1, n_dp):
             ids_copy(d, lax.rem(d + k, n_dp)).wait_send()
-            row_copy(d, lax.rem(d + k, n_dp)).wait_send()
+        for j in range(n_dp - 1):
+            row_copy(d, j).wait_send()
         for to in range(1, n_pp):
             e_copy(to).wait_send()
             over_copy(to).wait_send()
 
-    @pl.when(jnp.logical_not(is_last))
+    @pl.when(jnp.logical_not(is_last | lender))
     def _():
         for i in range(n_piece):
             x_copy(i).wait_send()
+
+    @pl.when(lender)
+    def _():
+        push_copy(0).wait_send()
+        push_copy(1).wait_send()
 
     @pl.when((p == 1) | (p == 3) | (p == 5))
     def _():
@@ -456,10 +514,8 @@
         in_specs=[vmem] * 5 + [anys] * 7,
         out_specs=(vmem, pl.BlockSpec(memory_space=pltpu.SMEM)),
         scratch_shapes=[
-            pltpu.VMEM((width, ffn), BF16),
-            pltpu.VMEM((ffn, width), BF16),
-            pltpu.VMEM((width, ffn), BF16),
-            pltpu.VMEM((ffn, width), BF16),
+            pltpu.VMEM((2, width, ffn), BF16),
+            pltpu.VMEM((2, ffn, width), BF16),
             pltpu.VMEM((2 * width, width), BF16),
             pltpu.VMEM((width, cols - ffn), BF16),
             pltpu.VMEM((n_dp, 1, seq + 2), jnp.int32),
@@ -480,6 +536,7 @@
             dma((8,)), dma((n_dp,)), dma((n_dp,)), dma((n_dp,)), dma((n_dp,)),
             dma((n_piece,)), dma((n_piece,)), dma((n_pp,)), dma(()), dma((4, n_piece)), dma((n_piece,)), dma((n_piece,)),
             dma((n_pp,)), dma((n_pp,)), dma((n_dp,)), dma((n_dp,)), dma((n_pp,)), dma(()), pltpu.SemaphoreType.REGULAR,
+            dma((2,)), dma((2,)),
         ],
         compiler_params=pltpu.CompilerParams(collective_id=0, has_side_effects=True, vmem_limit_bytes=VMEM_LIMIT),
         name="mtp_eval",

time: 95 us -> 88.9 us (0.936)
  Pallas kernels: 90.6 us -> 84.5 us
    pallas_call x1, Pallas kernels: 90.6 us -> 84.5 us  [mega(): pl.pallas_call(functools.partial(mega_kernel, n_dp, n_pp, seq, CAP), out_...]
where the time goes in v3:
time: 88.9 us; the launch traced here: 88.7 us
  Pallas kernels  84.5 us (95%)
  local copies, waits for them, and re-layouts  2.47 us (3%)
  between operations  1.42 us (2%)
    pallas_call x1, Pallas kernels, mega(): pl.pallas_call(functools.partial(mega_kernel, n_dp, n_pp, seq, CAP), out_...  84.5 us

profile of v3, /device:TPU:1, one launch (start us, length us, event | category | flops | bytes accessed | tf_op | source)
XLA Modules:
  0.0 88.7 jit_solution(15325577442246806351)
XLA Ops:
  0.6 0.0 copy-start.2
  0.6 0.0 copy-start.3
  0.7 0.0 copy-start.4
  0.7 0.0 copy-start.5
  0.7 0.0 copy-start.6
  0.7 84.5 %mtp_eval.1 = (f32[8,128]{1,0:T(8,128)}, s32[1,1]{1,0:T(1,128)}) custom-call(s32[1,1,130]{2,1,0:T(1,128)} %ids_ref.1, bf16[1024]{0:T(1024)(128)(2,1)} %gf_ref.1, bf16[1024]{0:T(1024)(128)(2,1)} %gh_ref.1, bf16[1024]{0:T(1024)(128)(2,1)} %ge_ref.1, bf16[1024]{0:T(1024)(128)(2,1)} %gm_ref.1, bf16[1,3144,1024]{2,1,0:T(8,128)(2,1)} %emb.1, ...), custom_call_target="tpu_custom_call" | custom-call | tf_op jit(solution)/shard_map/mtp_eval/pallas_call | solution.py:508
  85.9 0.0 copy-done.2
  85.9 0.0 copy-done.3
  85.9 0.0 copy-done.4
  86.0 0.0 copy-done.5
  86.0 0.0 copy-done.6
  86.0 0.3 conditional.1
  86.2 1.2 %slice.41 = f32[1,1]{1,0:T(1,128)} slice(f32[8,128]{1,0:T(8,128)} %get-tuple-element.510), slice={[2:3], [0:1]} | slice | bytes 8 | tf_op jit(solution)/shard_map/slice | solution.py:630
  87.4 1.3 %slice_bitcast_fusion = (f32[1,1,128]{2,1,0:T(1,128)}, f32[1,1,128]{2,1,0:T(1,128)}) fusion(f32[8,128]{1,0:T(8,128)} %get-tuple-element.510), kind=kLoop, calls=%fused_computation.121 | loop fusion | bytes 2048 | tf_op jit(solution)/shard_map/reshape | solution.py:630
Async XLA Ops:
  0.6 85.3 %copy-start.2 = (s32[1,1,130]{2,1,0:T(1,128)S(1)}, s32[1,1,130]{2,1,0:T(1,128)}, u32[]{:S(2)}) copy-start(s32[1,1,130]{2,1,0:T(1,128)} %ids_ref.1) | copy-start | bytes 1564
  0.6 85.3 %copy-start.3 = (bf16[1024]{0:T(1024)(128)(2,1)S(1)}, bf16[1024]{0:T(1024)(128)(2,1)}, u32[]{:S(2)}) copy-start(bf16[1024]{0:T(1024)(128)(2,1)} %gf_ref.1) | copy-start | bytes 6148
  0.7 85.3 %copy-start.4 = (bf16[1024]{0:T(1024)(128)(2,1)S(1)}, bf16[1024]{0:T(1024)(128)(2,1)}, u32[]{:S(2)}) copy-start(bf16[1024]{0:T(1024)(128)(2,1)} %gh_ref.1) | copy-start | bytes 6148
  0.7 85.3 %copy-start.5 = (bf16[1024]{0:T(1024)(128)(2,1)S(1)}, bf16[1024]{0:T(1024)(128)(2,1)}, u32[]{:S(2)}) copy-start(bf16[1024]{0:T(1024)(128)(2,1)} %ge_ref.1) | copy-start | bytes 6148
  0.7 85.3 %copy-start.6 = (bf16[1024]{0:T(1024)(128)(2,1)S(1)}, bf16[1024]{0:T(1024)(128)(2,1)}, u32[]{:S(2)}) copy-start(bf16[1024]{0:T(1024)(128)(2,1)} %gm_ref.1) | copy-start | bytes 6148

commit v4 on v3

--- a/solution.py
+++ b/solution.py
@@ -99,17 +99,26 @@
         pl.semaphore_signal(barrier, inc=1, device_id={"dp": lax.rem(d + k, n_dp)}, device_id_type=MESH)
     for k in range(1, n_pp):
         pl.semaphore_signal(barrier, inc=1, device_id={"pp": lax.rem(p + k, n_pp)}, device_id_type=MESH)
-    pl.semaphore_wait(barrier, n_dp - 1 + n_pp - 1)
+    @pl.when(even)
+    def _():
+        for k in range(1, n_dp):
+            pl.semaphore_signal(
+                barrier, inc=1, device_id={"dp": lax.rem(d + k, n_dp), "pp": lax.rem(p + 1, n_pp)}, device_id_type=MESH)
+
+    pl.semaphore_wait(barrier, n_pp - 1 + jnp.where(even, 1, 2) * (n_dp - 1))
 
     def ids_copy(owner, peer):
         return pltpu.make_async_remote_copy(
             src_ref=ids_ref.at[0], dst_ref=ids_all.at[owner], send_sem=ids_ss.at[peer], recv_sem=ids_rs.at[owner],
-            device_id={"dp": peer}, device_id_type=MESH)
-
-    @pl.when(is_first)
+            device_id={"dp": peer, "pp": 0}, device_id_type=MESH)
+
+    @pl.when(p == 1)
     def _():
         for k in range(1, n_dp):
             ids_copy(d, lax.rem(d + k, n_dp)).start()
+
+    @pl.when(is_first)
+    def _():
         ids_all[d] = ids_ref[0]
 
     @pl.when(lender)
@@ -228,8 +237,12 @@
             device_id={"pp": lax.rem(p + n_pp - 1, n_pp)}, device_id_type=MESH)
 
     def gelu_up(m, xn, slot):
-        for c in range(0, ffn, MLP_BLOCK):
-            hid[0:m, c:c + MLP_BLOCK] = jax.nn.gelu(dot32(xn, w1[slot, :, c:c + MLP_BLOCK])).astype(BF16)
+        n_blk = ffn // MLP_BLOCK
+        for b in range(n_blk + 1):
+            if b < n_blk:
+                lg[b % 2, 0:m, :] = dot32(xn, w1[slot, :, b * MLP_BLOCK:(b + 1) * MLP_BLOCK])
+            if b:
+                hid[0:m, (b - 1) * MLP_BLOCK:b * MLP_BLOCK] = jax.nn.gelu(lg[(b - 1) % 2, 0:m, :]).astype(BF16)
 
     def stage(turn, carry):
         lent = turn == 0
@@ -438,16 +451,19 @@
     ls_send[...] = both
     ls_recv[d] = both
 
-    def ls_copy(owner, peer):
-        return pltpu.make_async_remote_copy(
-            src_ref=ls_send, dst_ref=ls_recv.at[owner], send_sem=ls_ss.at[peer], recv_sem=ls_rs.at[owner],
-            device_id={"dp": peer}, device_id_type=MESH)
-
-    for k in range(1, n_dp):
-        ls_copy(d, lax.rem(d + k, n_dp)).start()
-    for k in range(1, n_dp):
-        peer = lax.rem(d + k, n_dp)
-        ls_copy(peer, peer).wait_recv()
+    def ls_copy(owner, peer, side):
+        return pltpu.make_async_remote_copy(
+            src_ref=ls_send, dst_ref=ls_recv.at[owner], send_sem=ls_ss.at[side, peer], recv_sem=ls_rs.at[owner],
+            device_id={"dp": peer, "pp": lax.rem(p + n_pp - side, n_pp)}, device_id_type=MESH)
+
+    @pl.when(jnp.logical_not(even))
+    def _():
+        for peer in order[:-1]:
+            ls_copy(d, peer, 1).start()
+            ls_copy(d, peer, 0).start()
+
+    for peer in order[:-1]:
+        ls_copy(peer, peer, 0).wait_recv()
     acc = ls_recv[0]
     for k in range(1, n_dp):
         acc = acc + ls_recv[k]
@@ -455,17 +471,24 @@
     out_ref[...] = jnp.where(sub == 0, main, jnp.where(sub == 1, mtp, jnp.broadcast_to(loss, (SUB, LANES))))
     flag_out[0, 0] = jnp.max(over_buf[1]).astype(jnp.int32)
 
-    for k in range(1, n_dp):
-        ls_copy(d, lax.rem(d + k, n_dp)).wait_send()
+    @pl.when(jnp.logical_not(even))
+    def _():
+        for peer in order[:-1]:
+            ls_copy(d, peer, 1).wait_send()
+            ls_copy(d, peer, 0).wait_send()
+
+    @pl.when(p == 1)
+    def _():
+        for k in range(1, n_dp):
+            ids_copy(d, lax.rem(d + k, n_dp)).wait_send()
+
     for k in range(1, n_pp):
         part_copy(p, lax.rem(p + k, n_pp)).wait_send()
 
     @pl.when(is_first)
     def _():
         for k in range(1, n_dp):
-            ids_copy(d, lax.rem(d + k, n_dp)).wait_send()
-        for j in range(n_dp - 1):
-            row_copy(d, j).wait_send()
+            row_copy(d, k - 1).wait_send()
         for to in range(1, n_pp):
             e_copy(to).wait_send()
             over_copy(to).wait_send()
@@ -535,7 +558,7 @@
             pltpu.VMEM((2, SUB, LANES), F32),
             dma((8,)), dma((n_dp,)), dma((n_dp,)), dma((n_dp,)), dma((n_dp,)),
             dma((n_piece,)), dma((n_piece,)), dma((n_pp,)), dma(()), dma((4, n_piece)), dma((n_piece,)), dma((n_piece,)),
-            dma((n_pp,)), dma((n_pp,)), dma((n_dp,)), dma((n_dp,)), dma((n_pp,)), dma(()), pltpu.SemaphoreType.REGULAR,
+            dma((n_pp,)), dma((n_pp,)), dma((2, n_dp)), dma((n_dp,)), dma((n_pp,)), dma(()), pltpu.SemaphoreType.REGULAR,
             dma((2,)), dma((2,)),
         ],
         compiler_params=pltpu.CompilerParams(collective_id=0, has_side_effects=True, vmem_limit_bytes=VMEM_LIMIT),
@@ -627,7 +650,7 @@
             return jnp.concatenate([main_nll, mtp_nll, jnp.broadcast_to(total, (SUB - 2, seq))], axis=0)
 
         packed = lax.cond(over[0, 0] > 0, slow, lambda: packed)
-        return packed[2, 0], packed[0:1].reshape(1, 1, seq), packed[1:2].reshape(1, 1, seq)
+        return jnp.max(packed[2]), packed[0:1].reshape(1, 1, seq), packed[1:2].reshape(1, 1, seq)
 
     rep = P()
     in_specs = (P(None, "dp", None), P("pp", "dp", None), P("pp"), P("pp"), rep, rep, rep, rep, rep, rep, rep, rep)

time: 88.9 us -> 86.6 us (0.974)
  local copies, waits for them, and re-layouts: 2.47 us -> 0.02 us
  other arithmetic: 0 us -> 1.9 us
  Pallas kernels: 84.5 us -> 82.8 us
    reshape x0 -> x1, other arithmetic: none -> 1.9 us  [body(): packed[1:2].reshape(1, 1, seq)]
    pallas_call x1, Pallas kernels: 84.5 us -> 82.8 us  [mega(): pl.pallas_call(functools.partial(mega_kernel, n_dp, n_pp, seq, CAP), out_...]
    reshape x1 -> x0, local copies, waits for them, and re-layouts: 1.27 us -> none  [body(): packed[1:2].reshape(1, 1, seq)]
    slice x1 -> x0, local copies, waits for them, and re-layouts: 1.19 us -> none  [body(): packed[2, 0]]
where the time goes in v4:
time: 86.6 us; the launch traced here: 86.4 us
  Pallas kernels  82.8 us (96%)
  other arithmetic  1.9 us (2%)
  between operations  1.42 us (2%)
    pallas_call x1, Pallas kernels, mega(): pl.pallas_call(functools.partial(mega_kernel, n_dp, n_pp, seq, CAP), out_...  82.8 us
    reshape x1, other arithmetic, body(): packed[1:2].reshape(1, 1, seq)  1.9 us

profile of v4, /device:TPU:1, one launch (start us, length us, event | category | flops | bytes accessed | tf_op | source)
XLA Modules:
  0.0 86.4 jit_solution(6315277240574671575)
XLA Ops:
  0.6 0.0 copy-start.2
  0.6 0.0 copy-start.3
  0.7 0.0 copy-start.4
  0.7 0.0 copy-start.5
  0.7 0.0 copy-start.6
  0.7 82.8 %mtp_eval.1 = (f32[8,128]{1,0:T(8,128)}, s32[1,1]{1,0:T(1,128)}) custom-call(s32[1,1,130]{2,1,0:T(1,128)} %ids_ref.1, bf16[1024]{0:T(1024)(128)(2,1)} %gf_ref.1, bf16[1024]{0:T(1024)(128)(2,1)} %gh_ref.1, bf16[1024]{0:T(1024)(128)(2,1)} %ge_ref.1, bf16[1024]{0:T(1024)(128)(2,1)} %gm_ref.1, bf16[1,3144,1024]{2,1,0:T(8,128)(2,1)} %emb.1, ...), custom_call_target="tpu_custom_call" | custom-call | tf_op jit(solution)/shard_map/mtp_eval/pallas_call | solution.py:531
  84.2 0.0 copy-done.2
  84.2 0.0 copy-done.3
  84.2 0.0 copy-done.4
  84.2 0.0 copy-done.5
  84.3 0.0 copy-done.6
  84.3 0.3 conditional.1
  84.5 1.9 %slice_bitcast_fusion = (f32[1,1,128]{2,1,0:T(1,128)}, f32[1,1,128]{2,1,0:T(1,128)}, f32[]{:T(128)}) fusion(f32[8,128]{1,0:T(8,128)} %get-tuple-element.511), kind=kLoop, calls=%fused_computation.121 | loop fusion | flops 127 | bytes 2564 | tf_op jit(solution)/shard_map/reshape | solution.py:653
Async XLA Ops:
  0.6 83.6 %copy-start.2 = (s32[1,1,130]{2,1,0:T(1,128)S(1)}, s32[1,1,130]{2,1,0:T(1,128)}, u32[]{:S(2)}) copy-start(s32[1,1,130]{2,1,0:T(1,128)} %ids_ref.1) | copy-start | bytes 1564
  0.6 83.6 %copy-start.3 = (bf16[1024]{0:T(1024)(128)(2,1)S(1)}, bf16[1024]{0:T(1024)(128)(2,1)}, u32[]{:S(2)}) copy-start(bf16[1024]{0:T(1024)(128)(2,1)} %gf_ref.1) | copy-start | bytes 6148
  0.7 83.6 %copy-start.4 = (bf16[1024]{0:T(1024)(128)(2,1)S(1)}, bf16[1024]{0:T(1024)(128)(2,1)}, u32[]{:S(2)}) copy-start(bf16[1024]{0:T(1024)(128)(2,1)} %gh_ref.1) | copy-start | bytes 6148
  0.7 83.6 %copy-start.5 = (bf16[1024]{0:T(1024)(128)(2,1)S(1)}, bf16[1024]{0:T(1024)(128)(2,1)}, u32[]{:S(2)}) copy-start(bf16[1024]{0:T(1024)(128)(2,1)} %ge_ref.1) | copy-start | bytes 6148
  0.7 83.6 %copy-start.6 = (bf16[1024]{0:T(1024)(128)(2,1)S(1)}, bf16[1024]{0:T(1024)(128)(2,1)}, u32[]{:S(2)}) copy-start(bf16[1024]{0:T(1024)(128)(2,1)} %gm_ref.1) | copy-start | bytes 6148

commit v5 on v4

--- a/solution.py
+++ b/solution.py
@@ -37,8 +37,9 @@
 
 def mega_kernel(
     n_dp, n_pp, seq, cap,
-    ids_ref, gf_ref, gh_ref, ge_ref, gm_ref, emb, w1h, w2h, wph, u1h, u2h, woh,
+    ids_hbm, gf_hbm, gh_hbm, ge_hbm, gm_hbm, emb, w1h, w2h, wph, u1h, u2h, woh,
     out_ref, flag_out,
+    ids_ref, gf_ref, gh_ref, ge_ref, gm_ref, flag_buf,
     w1, w2, wp, wo,
     ids_all, send_rows, recv_rows, xbuf, ybuf, xnb, hid, ebuf, hbuf, eall, zbuf, epart, xh, lg, mx, sm, pk,
     part_send, part_recv, ls_send, ls_recv, over_buf,
@@ -85,14 +86,10 @@
             src_ref=src.at[0, 0], dst_ref=dst.at[0], send_sem=push_ss.at[i], recv_sem=push_rs.at[i],
             device_id={"pp": lax.rem(p + 1, n_pp)}, device_id_type=MESH)
 
-    @pl.when(is_first)
-    def _():
-        tab_cp.start()
-
-    @pl.when(jnp.logical_not(even))
-    def _():
-        w1_cp.start()
-        w2_cp.start()
+    small = ((ids_hbm, ids_ref), (gf_hbm, gf_ref), (gh_hbm, gh_ref), (ge_hbm, ge_ref), (gm_hbm, gm_ref))
+    small_cp = [pltpu.make_async_copy(src, dst, wsem.at[8 + i]) for i, (src, dst) in enumerate(small)]
+    flag_cp = pltpu.make_async_copy(flag_buf, flag_out, wsem.at[13])
+    small_cp[0].start()
 
     barrier = pltpu.get_barrier_semaphore()
     for k in range(1, n_dp):
@@ -105,6 +102,20 @@
             pl.semaphore_signal(
                 barrier, inc=1, device_id={"dp": lax.rem(d + k, n_dp), "pp": lax.rem(p + 1, n_pp)}, device_id_type=MESH)
 
+    for cp in small_cp[1:]:
+        cp.start()
+
+    @pl.when(is_first)
+    def _():
+        tab_cp.start()
+
+    @pl.when(jnp.logical_not(even))
+    def _():
+        w1_cp.start()
+        w2_cp.start()
+
+    for cp in small_cp:
+        cp.wait()
     pl.semaphore_wait(barrier, n_pp - 1 + jnp.where(even, 1, 2) * (n_dp - 1))
 
     def ids_copy(owner, peer):
@@ -184,20 +195,20 @@
         key = jnp.where(valid, rank, -1.0)
         loc = jnp.where(valid, ids2 - low, 0).astype(F32)
         slot = iota((cap, n_id), 0).astype(F32)
-        for b in range(0, n_dp, 2):
-            picks = []
-            for s in (b, b + 1):
-                sel = key[s:s + 1, :] == slot
-                idx = jnp.sum(jnp.where(sel, loc[s:s + 1, :] + 1.0, 0.0), axis=1, keepdims=True) - 1.0
-                picks.append(idx)
-            idx2 = jnp.concatenate(picks, axis=0).astype(jnp.int32)
-            hot = jnp.where(iota((2 * cap, k_pad), 1) == idx2, 1.0, 0.0).astype(BF16)
-            w1[0, b * cap:(b + 2) * cap, 0:k_pad] = hot
         tab_cp.wait()
         blk = min(512, width)
         n_half = n_dp // 2
         for h in range(2):
             r0, r1 = h * n_half * cap, (h + 1) * n_half * cap
+            for b in range(h * n_half, (h + 1) * n_half, 2):
+                picks = []
+                for s in (b, b + 1):
+                    sel = key[s:s + 1, :] == slot
+                    idx = jnp.sum(jnp.where(sel, loc[s:s + 1, :] + 1.0, 0.0), axis=1, keepdims=True) - 1.0
+                    picks.append(idx)
+                idx2 = jnp.concatenate(picks, axis=0).astype(jnp.int32)
+                hot = jnp.where(iota((2 * cap, k_pad), 1) == idx2, 1.0, 0.0).astype(BF16)
+                w1[0, b * cap:(b + 2) * cap, 0:k_pad] = hot
             for c in range(0, width, blk):
                 tail = w2[0, k_main:k_pad, c:c + blk]
                 tail = jnp.where(iota((K_TILE, blk), 0) < n_rows - k_main, tail.astype(F32), 0.0).astype(BF16)
@@ -331,6 +342,9 @@
     def _():
         e_copy(1).wait_recv()
         over_copy(1).wait_recv()
+
+    flag_buf[0, 0] = jnp.max(over_buf[1]).astype(jnp.int32)
+    flag_cp.start()
 
     g_f, g_h, g_e, g_m = (ref[...].astype(F32).reshape(1, width) for ref in (gf_ref, gh_ref, ge_ref, gm_ref))
 
@@ -469,7 +483,7 @@
         acc = acc + ls_recv[k]
     loss = jnp.sum(acc, axis=1, keepdims=True) * (1.0 / (n_dp * seq))
     out_ref[...] = jnp.where(sub == 0, main, jnp.where(sub == 1, mtp, jnp.broadcast_to(loss, (SUB, LANES))))
-    flag_out[0, 0] = jnp.max(over_buf[1]).astype(jnp.int32)
+    flag_cp.wait()
 
     @pl.when(jnp.logical_not(even))
     def _():
@@ -534,9 +548,11 @@
             jax.ShapeDtypeStruct((SUB, LANES), F32),
             jax.ShapeDtypeStruct((1, 1), jnp.int32),
         ),
-        in_specs=[vmem] * 5 + [anys] * 7,
-        out_specs=(vmem, pl.BlockSpec(memory_space=pltpu.SMEM)),
+        in_specs=[anys] * 12,
+        out_specs=(vmem, anys),
         scratch_shapes=[
+            pltpu.VMEM((1, 1, seq + 2), jnp.int32), *[pltpu.VMEM((width,), BF16)] * 4,
+            pltpu.SMEM((1, 1), jnp.int32),
             pltpu.VMEM((2, width, ffn), BF16),
             pltpu.VMEM((2, ffn, width), BF16),
             pltpu.VMEM((2 * width, width), BF16),
@@ -556,7 +572,7 @@
             tile, pltpu.VMEM((n_pp, SUB, LANES), F32),
             tile, pltpu.VMEM((n_dp, SUB, LANES), F32),
             pltpu.VMEM((2, SUB, LANES), F32),
-            dma((8,)), dma((n_dp,)), dma((n_dp,)), dma((n_dp,)), dma((n_dp,)),
+            dma((14,)), dma((n_dp,)), dma((n_dp,)), dma((n_dp,)), dma((n_dp,)),
             dma((n_piece,)), dma((n_piece,)), dma((n_pp,)), dma(()), dma((4, n_piece)), dma((n_piece,)), dma((n_piece,)),
             dma((n_pp,)), dma((n_pp,)), dma((2, n_dp)), dma((n_dp,)), dma((n_pp,)), dma(()), pltpu.SemaphoreType.REGULAR,
             dma((2,)), dma((2,)),
@@ -647,10 +663,12 @@
         def slow():
             total, main_nll, mtp_nll = any_ids(
                 n_dp, n_pp, seq, tok_ids[0, 0], emb_s[0], w_one[0, 0], w_two[0, 0], *gains, w_proj, u_one, u_two, w_out)
-            return jnp.concatenate([main_nll, mtp_nll, jnp.broadcast_to(total, (SUB - 2, seq))], axis=0)
-
-        packed = lax.cond(over[0, 0] > 0, slow, lambda: packed)
-        return jnp.max(packed[2]), packed[0:1].reshape(1, 1, seq), packed[1:2].reshape(1, 1, seq)
+            return total, main_nll.reshape(1, 1, seq), mtp_nll.reshape(1, 1, seq)
+
+        def fast():
+            return jnp.max(packed[2]), packed[0:1].reshape(1, 1, seq), packed[1:2].reshape(1, 1, seq)
+
+        return lax.cond(over[0, 0] > 0, slow, fast)
 
     rep = P()
     in_specs = (P(None, "dp", None), P("pp", "dp", None), P("pp"), P("pp"), rep, rep, rep, rep, rep, rep, rep, rep)

time: 86.6 us -> 83.9 us (0.969)
  Pallas kernels: 82.8 us -> 81.2 us
    pallas_call x1, Pallas kernels: 82.8 us -> 81.2 us  [mega(): pl.pallas_call(functools.partial(mega_kernel, n_dp, n_pp, seq, CAP), out_...]
where the time goes in v5:
time: 83.9 us; the launch traced here: 83.8 us
  Pallas kernels  81.2 us (97%)
  between operations  1.41 us (2%)
  other arithmetic  1.12 us (1%)
    pallas_call x1, Pallas kernels, mega(): pl.pallas_call(functools.partial(mega_kernel, n_dp, n_pp, seq, CAP), out_...  81.2 us

profile of v5, /device:TPU:1, one launch (start us, length us, event | category | flops | bytes accessed | tf_op | source)
XLA Modules:
  0.0 83.8 jit_solution(15801178414289240327)
XLA Ops:
  0.6 0.0 copy-start.2
  0.6 0.0 copy-start.3
  0.7 0.0 copy-start.4
  0.7 0.0 copy-start.5
  0.7 0.0 copy-start.6
  0.7 81.2 %mtp_eval.1 = (f32[8,128]{1,0:T(8,128)S(1)}, s32[1,1]{1,0:T(1,128)}) custom-call(s32[1,1,130]{2,1,0:T(1,128)} %ids_hbm.1, bf16[1024]{0:T(1024)(128)(2,1)} %gf_hbm.1, bf16[1024]{0:T(1024)(128)(2,1)} %gh_hbm.1, bf16[1024]{0:T(1024)(128)(2,1)} %ge_hbm.1, bf16[1024]{0:T(1024)(128)(2,1)} %gm_hbm.1, bf16[1,3144,1024]{2,1,0:T(8,128)(2,1)} %emb.1, ...), custom_call_target="tpu_custom_call" | custom-call | tf_op jit(solution)/shard_map/mtp_eval/pallas_call | solution.py:545
  82.6 0.0 copy-done.2
  82.6 0.0 copy-done.3
  82.6 0.0 copy-done.4
  82.6 0.0 copy-done.5
  82.7 0.0 copy-done.6
  82.7 1.1 %conditional.1 = (f32[]{:T(128)}, f32[1,1,128]{2,1,0:T(1,128)}, f32[1,1,128]{2,1,0:T(1,128)}) conditional(s32[]{:T(128)} %bitcast.24, f32[8,128]{1,0:T(8,128)S(1)} %get-tuple-element.331, (bf16[1,3144,1024]{2,1,0:T(8,128)(2,1)}, s32[1,1,130]{2,1,0:T(1,128)S(1)}, bf16[1,1,1024,4096]{3,2,1,0:T(8,128)(2,1)}, bf16[1,1,4096,1024]{3,2,1,0:T(8,128)(2,1)}, ...), branch_computations={%region_0.0_spmd, %region_2.22_spmd} | conditional | flops 31260002304 | bytes 424958944 | solution.py:671
  82.7 1.1 %slice_bitcast_fusion = (f32[1,1,128]{2,1,0:T(1,128)}, f32[1,1,128]{2,1,0:T(1,128)}, f32[]{:T(128)}) fusion(f32[8,128]{1,0:T(8,128)S(1)} %param), kind=kLoop, calls=%fused_computation.4 | loop fusion | flops 127 | bytes 2564 | tf_op jit(solution)/shard_map/cond/branch_0_fun/reshape | solution.py:669
Async XLA Ops:
  0.6 82.0 %copy-start.2 = (s32[1,1,130]{2,1,0:T(1,128)S(1)}, s32[1,1,130]{2,1,0:T(1,128)}, u32[]{:S(2)}) copy-start(s32[1,1,130]{2,1,0:T(1,128)} %ids_hbm.1) | copy-start | bytes 1564
  0.6 82.0 %copy-start.3 = (bf16[1024]{0:T(1024)(128)(2,1)S(1)}, bf16[1024]{0:T(1024)(128)(2,1)}, u32[]{:S(2)}) copy-start(bf16[1024]{0:T(1024)(128)(2,1)} %gf_hbm.1) | copy-start | bytes 6148
  0.7 82.0 %copy-start.4 = (bf16[1024]{0:T(1024)(128)(2,1)S(1)}, bf16[1024]{0:T(1024)(128)(2,1)}, u32[]{:S(2)}) copy-start(bf16[1024]{0:T(1024)(128)(2,1)} %gh_hbm.1) | copy-start | bytes 6148
  0.7 82.0 %copy-start.5 = (bf16[1024]{0:T(1024)(128)(2,1)S(1)}, bf16[1024]{0:T(1024)(128)(2,1)}, u32[]{:S(2)}) copy-start(bf16[1024]{0:T(1024)(128)(2,1)} %ge_hbm.1) | copy-start | bytes 6148
  0.7 82.0 %copy-start.6 = (bf16[1024]{0:T(1024)(128)(2,1)S(1)}, bf16[1024]{0:T(1024)(128)(2,1)}, u32[]{:S(2)}) copy-start(bf16[1024]{0:T(1024)(128)(2,1)} %gm_hbm.1) | copy-start | bytes 6148

commit v6 on v5

--- a/solution.py
+++ b/solution.py
@@ -35,20 +35,27 @@
     return jnp.dot(a, b, preferred_element_type=F32)
 
 
+def shard_tiles(n_tiles, ffn):
+    pair, kept = n_tiles // 2, ffn // LANES
+    step = MLP_BLOCK // LANES
+    even_tiles = kept + ((pair // 2 - kept) // step - 1) * step
+    return even_tiles, n_tiles - pair - even_tiles
+
+
 def mega_kernel(
     n_dp, n_pp, seq, cap,
     ids_hbm, gf_hbm, gh_hbm, ge_hbm, gm_hbm, emb, w1h, w2h, wph, u1h, u2h, woh,
     out_ref, flag_out,
     ids_ref, gf_ref, gh_ref, ge_ref, gm_ref, flag_buf,
     w1, w2, wp, wo,
-    ids_all, send_rows, recv_rows, xbuf, ybuf, xnb, hid, ebuf, hbuf, eall, zbuf, epart, xh, lg, mx, sm, pk,
+    ids_all, picked, send_rows, recv_rows, xs, xnb, hid, ebuf, hbuf, eall, zbuf, epart, xh, lg, mx, sm, pk,
     part_send, part_recv, ls_send, ls_recv, over_buf,
     wsem, ids_ss, ids_rs, row_ss, row_rs, x_ss, x_rs, e_ss, e_rs, h_ss, h_rs, f_ss, part_ss, part_rs, ls_ss, ls_rs,
     over_ss, over_rs, link_free, push_ss, push_rs,
 ):
     d = lax.axis_index("dp")
     p = lax.axis_index("pp")
-    width = xbuf.shape[1]
+    width = xs.shape[2]
     ffn = w1.shape[2]
     n_rows = emb.shape[1]
     half = seq // 2
@@ -56,9 +63,11 @@
     shard = lax.rem(p, n_shard)
     group = p // n_shard
     n_tiles = woh.shape[1] // LANES
-    base_tiles = n_tiles // n_shard
-    cols = ffn + wo.shape[1]
+    even_tiles, odd_tiles = shard_tiles(n_tiles, ffn)
+    tile0 = (shard // 2) * (n_tiles // 2) + lax.rem(shard, 2) * even_tiles
+    cols = odd_tiles * LANES
     own_cols = wo.shape[1]
+    even_cols = even_tiles * LANES - ffn
     n_piece = width // PIECE
     is_first = p == 0
     is_last = p == n_pp - 1
@@ -70,14 +79,16 @@
     n_id = seq + 2
     n_slots = n_dp * cap
 
-    col0 = pl.multiple_of(shard * (base_tiles * LANES), LANES)
+    col0 = pl.multiple_of(tile0 * LANES, LANES)
     tab_cp = pltpu.make_async_copy(emb.at[0], w2.at[0, pl.ds(0, n_rows), :], wsem.at[0])
     w1_cp = pltpu.make_async_copy(w1h.at[0, 0], w1.at[1], wsem.at[1])
     w2_cp = pltpu.make_async_copy(w2h.at[0, 0], w2.at[1], wsem.at[2])
     u1_cp = pltpu.make_async_copy(u1h, w1.at[0], wsem.at[3])
     u2_cp = pltpu.make_async_copy(u2h, w2.at[0], wsem.at[4])
     wp_cp = pltpu.make_async_copy(wph, wp, wsem.at[5])
-    wo_cp = pltpu.make_async_copy(woh.at[:, pl.ds(col0 + ffn, own_cols)], wo, wsem.at[6])
+    wo_even_cp = pltpu.make_async_copy(
+        woh.at[:, pl.ds(col0 + ffn, even_cols)], wo.at[:, pl.ds(0, even_cols)], wsem.at[6])
+    wo_odd_cp = pltpu.make_async_copy(woh.at[:, pl.ds(col0 + ffn, own_cols)], wo, wsem.at[6])
     late_cp = pltpu.make_async_copy(woh.at[:, pl.ds(col0, ffn)], w1.at[1], wsem.at[7])
 
     def push_copy(i):
@@ -148,7 +159,14 @@
     @pl.when(jnp.logical_not(is_first))
     def _():
         wp_cp.start()
-        wo_cp.start()
+
+    @pl.when(lender)
+    def _():
+        wo_even_cp.start()
+
+    @pl.when(jnp.logical_not(even))
+    def _():
+        wo_odd_cp.start()
 
     n_y = 4
     n_z = n_dp // n_y
@@ -194,42 +212,52 @@
         rank = dot32(jnp.where(valid, 1.0, 0.0).astype(BF16), before)
         key = jnp.where(valid, rank, -1.0)
         loc = jnp.where(valid, ids2 - low, 0).astype(F32)
+        picked[0] = key
+        picked[1] = loc + 1.0
         slot = iota((cap, n_id), 0).astype(F32)
         tab_cp.wait()
+        tail = w2[0, k_main:k_pad, :]
+        w2[0, k_main:k_pad, :] = jnp.where(iota((K_TILE, width), 0) < n_rows - k_main, tail.astype(F32), 0.0).astype(BF16)
         blk = min(512, width)
-        n_half = n_dp // 2
-        for h in range(2):
-            r0, r1 = h * n_half * cap, (h + 1) * n_half * cap
-            for b in range(h * n_half, (h + 1) * n_half, 2):
-                picks = []
+        n_grp = 4
+
+        def select(g, carry):
+            row0 = pl.multiple_of(g * (n_grp * cap), 2 * SUB)
+            for b in range(0, n_grp, 2):
+                ids_at = []
                 for s in (b, b + 1):
-                    sel = key[s:s + 1, :] == slot
-                    idx = jnp.sum(jnp.where(sel, loc[s:s + 1, :] + 1.0, 0.0), axis=1, keepdims=True) - 1.0
-                    picks.append(idx)
-                idx2 = jnp.concatenate(picks, axis=0).astype(jnp.int32)
+                    sel = picked[0, pl.ds(g * n_grp + s, 1), :] == slot
+                    idx = jnp.sum(jnp.where(sel, picked[1, pl.ds(g * n_grp + s, 1), :], 0.0), axis=1, keepdims=True) - 1.0
+                    ids_at.append(idx)
+                idx2 = jnp.concatenate(ids_at, axis=0).astype(jnp.int32)
                 hot = jnp.where(iota((2 * cap, k_pad), 1) == idx2, 1.0, 0.0).astype(BF16)
-                w1[0, b * cap:(b + 2) * cap, 0:k_pad] = hot
+                w1[0, pl.ds(row0 + b * cap, 2 * cap), 0:k_pad] = hot
             for c in range(0, width, blk):
-                tail = w2[0, k_main:k_pad, c:c + blk]
-                tail = jnp.where(iota((K_TILE, blk), 0) < n_rows - k_main, tail.astype(F32), 0.0).astype(BF16)
-                got = dot32(w1[0, r0:r1, 0:k_main], w2[0, 0:k_main, c:c + blk]) + dot32(w1[0, r0:r1, k_main:k_pad], tail)
-                for s in range(n_half):
-                    send_rows[h * n_half + s, :, c:c + blk] = got[s * cap:(s + 1) * cap, :].astype(BF16)
-            for j in range(h * n_half, min((h + 1) * n_half, n_dp - 1)):
-                row_copy(d, j).start()
+                got = dot32(w1[0, pl.ds(row0, n_grp * cap), 0:k_pad], w2[0, 0:k_pad, c:c + blk])
+                for s in range(n_grp):
+                    send_rows[g * n_grp + s, :, c:c + blk] = got[s * cap:(s + 1) * cap, :].astype(BF16)
+            for at in range(n_dp // n_grp):
+                @pl.when(g == at)
+                def _():
+                    for j in range(at * n_grp, min((at + 1) * n_grp, n_dp - 1)):
+                        row_copy(d, j).start()
+
+            return carry
+
+        lax.fori_loop(0, n_dp // n_grp, select, 0)
         recv_rows[d] = send_rows[n_dp - 1]
         u1_cp.start()
         u2_cp.start()
         wp_cp.start()
-        wo_cp.start()
+        wo_even_cp.start()
         for j in range(n_dp - 1):
             row_copy(order[j], j).wait_recv()
-        xbuf[...] = dot32(xnb[:, 0:n_slots], recv_rows[...].reshape(n_slots, width)).astype(BF16)
+        xs[1] = dot32(xnb[:, 0:n_slots], recv_rows[...].reshape(n_slots, width)).astype(BF16)
 
     def x_copy(i):
         part = pl.ds(i * PIECE, PIECE)
         return pltpu.make_async_remote_copy(
-            src_ref=ybuf.at[:, part], dst_ref=xbuf.at[:, part], send_sem=x_ss.at[i], recv_sem=x_rs.at[i],
+            src_ref=xs.at[2, :, part], dst_ref=xs.at[jnp.where(is_first, 1, 0), :, part], send_sem=x_ss.at[i], recv_sem=x_rs.at[i],
             device_id={"pp": jnp.where(is_first, 1, lax.rem(p + 2, n_pp))}, device_id_type=MESH)
 
     h_peers = ((3, 0), (1, 0), (5, half), (6, half))
@@ -238,7 +266,7 @@
         to, row0 = h_peers[j]
         part = pl.ds(i * PIECE, PIECE)
         return pltpu.make_async_remote_copy(
-            src_ref=ybuf.at[pl.ds(row0, half), part], dst_ref=hbuf.at[:, part], send_sem=h_ss.at[j, i], recv_sem=h_rs.at[i],
+            src_ref=xs.at[2, pl.ds(row0, half), part], dst_ref=hbuf.at[:, part], send_sem=h_ss.at[j, i], recv_sem=h_rs.at[i],
             device_id={"pp": to}, device_id_type=MESH)
 
     def f_copy(i):
@@ -279,12 +307,12 @@
             def _():
                 pl.semaphore_signal(link_free, inc=1, device_id={"pp": 0}, device_id_type=MESH)
 
-            xnb[...] = norm_f32(xbuf[...].astype(F32)).astype(BF16)
+            xnb[...] = norm_f32(xs[turn].astype(F32)).astype(BF16)
             gelu_up(seq, xnb[...], turn)
             for i in range(n_piece):
                 c = i * PIECE
-                out = xbuf[:, c:c + PIECE].astype(F32) + dot32(hid[...], w2[turn, :, c:c + PIECE])
-                ybuf[:, c:c + PIECE] = out.astype(BF16)
+                out = xs[turn, :, c:c + PIECE].astype(F32) + dot32(hid[...], w2[turn, :, c:c + PIECE])
+                xs[turn + 1, :, c:c + PIECE] = out.astype(BF16)
 
                 @pl.when(jnp.logical_not(lent | is_last))
                 def _():
@@ -299,7 +327,6 @@
             def _():
                 u1_cp.start()
                 u2_cp.start()
-                xbuf[...] = ybuf[...]
 
             @pl.when(jnp.logical_not(lent))
             def _():
@@ -353,18 +380,26 @@
     epart[...] = dot32(e_n, wp[width:2 * width, :])
     u1_cp.wait()
     u2_cp.wait()
-    wo_cp.wait()
+
+    @pl.when(even)
+    def _():
+        wo_even_cp.wait()
+
+    @pl.when(jnp.logical_not(even))
+    def _():
+        wo_odd_cp.wait()
+
 
     row_f = jnp.broadcast_to(ids_ref[0], (2 * half, n_id))
     rr = iota((2 * half, n_id), 0)
     at = jnp.where(rr < half, rr + 1, rr - half + 2) + group * half
     tgt = jnp.sum(jnp.where(iota((2 * half, n_id), 1) == at, row_f, 0).astype(F32), axis=1, keepdims=True)
-    tgt = tgt.astype(jnp.int32) - shard * (base_tiles * LANES)
+    tgt = tgt.astype(jnp.int32) - tile0 * LANES
     tgt = jnp.broadcast_to(tgt, (2 * half, LANES))
 
     @pl.when(is_last)
     def _():
-        hbuf[...] = ybuf[half:seq, :]
+        hbuf[...] = xs[2, half:seq, :]
 
     @pl.when(jnp.logical_not(is_last))
     def _():
@@ -386,8 +421,11 @@
 
     lane = iota((2 * half, LANES), 1)
     tail_ok = jnp.broadcast_to(shard == n_shard - 1, (2 * half, LANES))
-    blocks = [(wo, c, ffn + c, min(MLP_BLOCK, own_cols - c)) for c in range(0, own_cols, MLP_BLOCK)]
+    blocks = [(wo, c, ffn + c, MLP_BLOCK) for c in range(0, even_cols, MLP_BLOCK)]
+    n_early = len(blocks)
     blocks += [(w1.at[1], c, c, MLP_BLOCK) for c in range(0, ffn, MLP_BLOCK)]
+    n_both = len(blocks)
+    blocks += [(wo, c, ffn + c, min(MLP_BLOCK, own_cols - c)) for c in range(even_cols, own_cols, MLP_BLOCK)]
 
     def logits_of(i):
         ref, c, _, n = blocks[i]
@@ -417,13 +455,21 @@
         sm[...] = total
         pk[...] = hit
 
-    for i in range(len(blocks)):
-        if i == len(blocks) - ffn // MLP_BLOCK:
+    for i in range(n_both):
+        if i == n_early:
             late_cp.wait()
         logits_of(i)
         if i:
             fold(i - 1)
-    fold(len(blocks) - 1)
+    fold(n_both - 1)
+
+    @pl.when(jnp.logical_not(even))
+    def _():
+        for i in range(n_both, len(blocks)):
+            logits_of(i)
+            if i > n_both:
+                fold(i - 1)
+        fold(len(blocks) - 1)
 
     eye = iota((2 * half, LANES), 0) == iota((2 * half, LANES), 1)
 
@@ -531,9 +577,7 @@
 
 def mega(n_dp, n_pp, seq, ids, gains, emb, w1, w2, wp, u1, u2, wo):
     width, ffn = w1.shape[2], w1.shape[3]
-    n_tiles = wo.shape[1] // LANES
-    n_shard = n_pp // 2
-    cols = (n_tiles - (n_shard - 1) * (n_tiles // n_shard)) * LANES
+    cols = shard_tiles(wo.shape[1] // LANES, ffn)[1] * LANES
     half = seq // 2
     n_piece = width // PIECE
     dma = pltpu.SemaphoreType.DMA
@@ -558,9 +602,10 @@
             pltpu.VMEM((2 * width, width), BF16),
             pltpu.VMEM((width, cols - ffn), BF16),
             pltpu.VMEM((n_dp, 1, seq + 2), jnp.int32),
+            pltpu.VMEM((2, n_dp, seq + 2), F32),
             pltpu.VMEM((n_dp, CAP, width), BF16),
             pltpu.VMEM((n_dp, CAP, width), BF16),
-            act, act, act,
+            pltpu.VMEM((3, seq, width), BF16), act,
             pltpu.VMEM((seq, ffn), BF16),
             act_half, act_half,
             act,
@@ -668,7 +713,7 @@
         def fast():
             return jnp.max(packed[2]), packed[0:1].reshape(1, 1, seq), packed[1:2].reshape(1, 1, seq)
 
-        return lax.cond(over[0, 0] > 0, slow, fast)
+        return lax.switch(over[0, 0], [fast, slow])
 
     rep = P()
     in_specs = (P(None, "dp", None), P("pp", "dp", None), P("pp"), P("pp"), rep, rep, rep, rep, rep, rep, rep, rep)

time: 83.9 us -> 83.4 us (level)
  no operation moved by 1% of the time
where the time goes in v6:
time: 83.4 us; the launch traced here: 83.3 us
  Pallas kernels  80.8 us (97%)
  between operations  1.41 us (2%)
  other arithmetic  1.12 us (1%)
    pallas_call x1, Pallas kernels, mega(): pl.pallas_call(functools.partial(mega_kernel, n_dp, n_pp, seq, CAP), out_...  80.8 us

profile of v6, /device:TPU:1, one launch (start us, length us, event | category | flops | bytes accessed | tf_op | source)
XLA Modules:
  0.0 83.3 jit_solution(14504633376780950586)
XLA Ops:
  0.6 0.0 copy-start.2
  0.6 0.0 copy-start.3
  0.7 0.0 copy-start.4
  0.7 0.0 copy-start.5
  0.7 0.0 copy-start.6
  0.7 80.8 %mtp_eval.1 = (f32[8,128]{1,0:T(8,128)S(1)}, s32[1,1]{1,0:T(1,128)}) custom-call(s32[1,1,130]{2,1,0:T(1,128)} %ids_hbm.1, bf16[1024]{0:T(1024)(128)(2,1)} %gf_hbm.1, bf16[1024]{0:T(1024)(128)(2,1)} %gh_hbm.1, bf16[1024]{0:T(1024)(128)(2,1)} %ge_hbm.1, bf16[1024]{0:T(1024)(128)(2,1)} %gm_hbm.1, bf16[1,3144,1024]{2,1,0:T(8,128)(2,1)} %emb.1, ...), custom_call_target="tpu_custom_call" | custom-call | tf_op jit(solution)/shard_map/mtp_eval/pallas_call | solution.py:589
  82.1 0.0 copy-done.2
  82.1 0.0 copy-done.3
  82.2 0.0 copy-done.4
  82.2 0.0 copy-done.5
  82.2 0.0 copy-done.6
  82.2 1.1 %conditional.1 = (f32[]{:T(128)}, f32[1,1,128]{2,1,0:T(1,128)}, f32[1,1,128]{2,1,0:T(1,128)}) conditional(s32[]{:T(128)} %bitcast.24, f32[8,128]{1,0:T(8,128)S(1)} %get-tuple-element.331, (bf16[1,3144,1024]{2,1,0:T(8,128)(2,1)}, s32[1,1,130]{2,1,0:T(1,128)S(1)}, bf16[1,1,1024,4096]{3,2,1,0:T(8,128)(2,1)}, bf16[1,1,4096,1024]{3,2,1,0:T(8,128)(2,1)}, ...), branch_computations={%region_0.0_spmd, %region_2.22_spmd} | conditional | flops 31260002304 | bytes 424958944 | solution.py:716
  82.2 1.1 %slice_bitcast_fusion = (f32[1,1,128]{2,1,0:T(1,128)}, f32[1,1,128]{2,1,0:T(1,128)}, f32[]{:T(128)}) fusion(f32[8,128]{1,0:T(8,128)S(1)} %param), kind=kLoop, calls=%fused_computation.4 | loop fusion | flops 127 | bytes 2564 | tf_op jit(solution)/shard_map/cond/branch_0_fun/reshape | solution.py:714
Async XLA Ops:
  0.6 81.5 %copy-start.2 = (s32[1,1,130]{2,1,0:T(1,128)S(1)}, s32[1,1,130]{2,1,0:T(1,128)}, u32[]{:S(2)}) copy-start(s32[1,1,130]{2,1,0:T(1,128)} %ids_hbm.1) | copy-start | bytes 1564
  0.6 81.5 %copy-start.3 = (bf16[1024]{0:T(1024)(128)(2,1)S(1)}, bf16[1024]{0:T(1024)(128)(2,1)}, u32[]{:S(2)}) copy-start(bf16[1024]{0:T(1024)(128)(2,1)} %gf_hbm.1) | copy-start | bytes 6148
  0.7 81.5 %copy-start.4 = (bf16[1024]{0:T(1024)(128)(2,1)S(1)}, bf16[1024]{0:T(1024)(128)(2,1)}, u32[]{:S(2)}) copy-start(bf16[1024]{0:T(1024)(128)(2,1)} %gh_hbm.1) | copy-start | bytes 6148
  0.7 81.5 %copy-start.5 = (bf16[1024]{0:T(1024)(128)(2,1)S(1)}, bf16[1024]{0:T(1024)(128)(2,1)}, u32[]{:S(2)}) copy-start(bf16[1024]{0:T(1024)(128)(2,1)} %ge_hbm.1) | copy-start | bytes 6148
  0.7 81.5 %copy-start.6 = (bf16[1024]{0:T(1024)(128)(2,1)S(1)}, bf16[1024]{0:T(1024)(128)(2,1)}, u32[]{:S(2)}) copy-start(bf16[1024]{0:T(1024)(128)(2,1)} %gm_hbm.1) | copy-start | bytes 6148
